TPU v7x, 128 devices: a whole 4x4x4 slice. The times are simulated.
128 devices in a mesh: batch: 1, col: 16 (over z, y), row: 8 (over x, core).
Axes of the slice: x: 4, y: 4, z: 4, core: 2. Of those that a mesh axis runs over, the one named last changes fastest.
Arguments:
- tri_mat: float32 [8192, 8192], P(('batch', 'row'), 'col')
Outputs:
- output: float32 [8192, 8192], P(('batch', 'row'), 'col')
All inputs are finite; a program needn't handle non-finite values.
Results may differ from a plain program's by a relative error of at most 0.001.
Values sent between devices are 32-bit elements.
A program may use at most 1 GiB of HBM per device.

v0:
```python
import jax
import jax.numpy as jnp
from jax import lax
from jax.sharding import PartitionSpec as P

LEAF_MAX = 512


def mat_prod(left_mat, right_mat):
    return jnp.dot(left_mat, right_mat, precision=lax.Precision.HIGHEST, preferred_element_type=jnp.float32)


def take_half(local_tile, axis_name, axis_len, tile_dim, second):
    half_len = local_tile.shape[tile_dim] // 2
    halves = [lax.slice_in_dim(local_tile, 0, half_len, axis=tile_dim), lax.slice_in_dim(local_tile, half_len, 2 * half_len, axis=tile_dim)]
    offset = axis_len if second else 0
    if axis_len == 1:
        return halves[offset]
    received = []
    for half_idx in range(2):
        pair_list = [((offset + dest_idx) // 2, dest_idx) for dest_idx in range(axis_len) if (offset + dest_idx) % 2 == half_idx]
        received.append(lax.ppermute(halves[half_idx], axis_name, pair_list))
    axis_pos = lax.axis_index(axis_name)
    return jnp.where((offset + axis_pos) % 2 == 0, received[0], received[1])


def put_half(local_tile, axis_name, axis_len, tile_dim, second):
    offset = axis_len if second else 0
    if axis_len == 1:
        zero_tile = jnp.zeros_like(local_tile)
        pieces = [zero_tile, local_tile] if second else [local_tile, zero_tile]
        return jnp.concatenate(pieces, axis=tile_dim)
    slot_list = []
    for slot_idx in range(2):
        pair_list = [(src_idx, (offset + src_idx) // 2) for src_idx in range(axis_len) if (offset + src_idx) % 2 == slot_idx]
        slot_list.append(lax.ppermute(local_tile, axis_name, pair_list))
    return jnp.concatenate(slot_list, axis=tile_dim)


def summa_prod(left_tile, right_tile):
    left_rows = lax.all_gather(left_tile, "col", axis=1, tiled=True)
    right_cols = lax.all_gather(right_tile, "row", axis=0, tiled=True)
    return mat_prod(left_rows, right_cols)


def leaf_inverse(local_tile):
    row_panel = lax.all_gather(local_tile, "row", axis=0, tiled=True)
    leaf_mat = lax.all_gather(row_panel, "col", axis=1, tiled=True)
    leaf_size = leaf_mat.shape[0]
    tile_rows, tile_cols = local_tile.shape
    col_start = lax.axis_index("col") * tile_cols
    eye_cols = (jnp.arange(leaf_size)[:, None] == jnp.arange(tile_cols)[None, :] + col_start).astype(jnp.float32)
    solved = lax.linalg.triangular_solve(leaf_mat, eye_cols, left_side=True, lower=True)
    return lax.dynamic_slice_in_dim(solved, lax.axis_index("row") * tile_rows, tile_rows, axis=0)


def invert_tile(local_tile, rows_n, cols_n):
    if local_tile.shape[0] * rows_n <= LEAF_MAX:
        return leaf_inverse(local_tile)
    left_cols = take_half(local_tile, "col", cols_n, 1, False)
    block_a = take_half(left_cols, "row", rows_n, 0, False)
    block_c = take_half(left_cols, "row", rows_n, 0, True)
    bottom_rows = take_half(local_tile, "row", rows_n, 0, True)
    block_b = take_half(bottom_rows, "col", cols_n, 1, True)
    inv_a = invert_tile(block_a, rows_n, cols_n)
    inv_b = invert_tile(block_b, rows_n, cols_n)
    cross_prod = summa_prod(block_c, inv_a)
    lower_left = -summa_prod(inv_b, cross_prod)
    top_half = put_half(inv_a, "col", cols_n, 1, False)
    bottom_half = put_half(lower_left, "col", cols_n, 1, False) + put_half(inv_b, "col", cols_n, 1, True)
    return put_half(top_half, "row", rows_n, 0, False) + put_half(bottom_half, "row", rows_n, 0, True)


def solution(mesh):
    rows_n = mesh.shape["row"]
    cols_n = mesh.shape["col"]
    tile_spec = P(("batch", "row"), "col")

    def local_fn(local_tile):
        return invert_tile(local_tile, rows_n, cols_n)

    return jax.shard_map(local_fn, mesh=mesh, in_specs=(tile_spec,), out_specs=tile_spec, check_vma=False)
```

profile of v0, /device:TPU:38, one launch (start us, length us, event | category | flops | bytes accessed | tf_op | source)
XLA Modules:
  0.0 3239.6 jit_solution(9489647766918247504)
XLA Ops:
  15.5 22.7 collective-permute-done
  40.6 13.7 collective-permute-done.2
  119.4 19.2 all-gather.5
  286.7 13.4 all-gather.21
  498.5 13.3 all-gather.13
  619.1 12.9 all-gather.24
  665.1 13.4 all-gather.29
  726.7 13.1 all-gather.28
  756.1 24.1 all_gather.293
  784.2 23.7 all_gather.281
  808.0 21.1 all_gather.289
  838.7 39.3 %custom-call.21 = f32[4,128,128]{1,2,0:T(8,128)S(1)} custom-call(f32[4,128,128]{2,1,0:T(8,128)S(1)} %get-tuple-element.107), custom_call_target="InvertDiagBlocksLowerTriangular" | custom-call | tf_op jit(solution)/shard_map/triangular_solve/custom-call.1 | solution.py:53
  885.2 24.0 all_gather.288
  918.2 39.3 %custom-call.20 = f32[4,128,128]{1,2,0:T(8,128)S(1)} custom-call(f32[4,128,128]{2,1,0:T(8,128)S(1)} %get-tuple-element.106), custom_call_target="InvertDiagBlocksLowerTriangular" | custom-call | tf_op jit(solution)/shard_map/triangular_solve/custom-call.1 | solution.py:53
  1000.9 39.3 %custom-call.19 = f32[4,128,128]{1,2,0:T(8,128)S(1)} custom-call(f32[4,128,128]{2,1,0:T(8,128)S(1)} %get-tuple-element.105), custom_call_target="InvertDiagBlocksLowerTriangular" | custom-call | tf_op jit(solution)/shard_map/triangular_solve/custom-call.1 | solution.py:53
  1057.1 39.3 %custom-call.18 = f32[4,128,128]{1,2,0:T(8,128)S(1)} custom-call(f32[4,128,128]{2,1,0:T(8,128)S(1)} %get-tuple-element.104), custom_call_target="InvertDiagBlocksLowerTriangular" | custom-call | tf_op jit(solution)/shard_map/triangular_solve/custom-call.1 | solution.py:53
  1123.9 20.6 all_gather.280
  1207.3 14.6 all_gather.294
  1222.3 12.8 all_gather.295
  1235.2 22.7 all_gather.292
  1294.2 24.3 all_gather.313
  1318.5 23.4 all_gather.337
  1345.3 22.0 all_gather.357
  1375.1 22.8 all_gather.301
  1401.2 21.6 all_gather.309
  1426.1 22.8 all_gather.345
  1450.9 21.6 all_gather.353
  1472.6 22.8 all_gather.325
  1495.4 21.6 all_gather.333
  1527.2 39.3 %custom-call.29 = f32[4,128,128]{1,2,0:T(8,128)S(1)} custom-call(f32[4,128,128]{2,1,0:T(8,128)S(1)} %get-tuple-element.115), custom_call_target="InvertDiagBlocksLowerTriangular" | custom-call | tf_op jit(solution)/shard_map/triangular_solve/custom-call.1 | solution.py:53
  1575.5 23.3 all_gather.332
  1608.4 39.3 %custom-call.28 = f32[4,128,128]{1,2,0:T(8,128)S(1)} custom-call(f32[4,128,128]{2,1,0:T(8,128)S(1)} %get-tuple-element.114), custom_call_target="InvertDiagBlocksLowerTriangular" | custom-call | tf_op jit(solution)/shard_map/triangular_solve/custom-call.1 | solution.py:53
  1692.4 39.3 %custom-call.27 = f32[4,128,128]{1,2,0:T(8,128)S(1)} custom-call(f32[4,128,128]{2,1,0:T(8,128)S(1)} %get-tuple-element.113), custom_call_target="InvertDiagBlocksLowerTriangular" | custom-call | tf_op jit(solution)/shard_map/triangular_solve/custom-call.1 | solution.py:53
  1740.3 21.9 all_gather.324
  1772.9 39.3 %custom-call.23 = f32[4,128,128]{1,2,0:T(8,128)S(1)} custom-call(f32[4,128,128]{2,1,0:T(8,128)S(1)} %get-tuple-element.109), custom_call_target="InvertDiagBlocksLowerTriangular" | custom-call | tf_op jit(solution)/shard_map/triangular_solve/custom-call.1 | solution.py:53
  1823.7 39.3 %custom-call.22 = f32[4,128,128]{1,2,0:T(8,128)S(1)} custom-call(f32[4,128,128]{2,1,0:T(8,128)S(1)} %get-tuple-element.108), custom_call_target="InvertDiagBlocksLowerTriangular" | custom-call | tf_op jit(solution)/shard_map/triangular_solve/custom-call.1 | solution.py:53
  1874.0 39.3 %custom-call.25 = f32[4,128,128]{1,2,0:T(8,128)S(1)} custom-call(f32[4,128,128]{2,1,0:T(8,128)S(1)} %get-tuple-element.111), custom_call_target="InvertDiagBlocksLowerTriangular" | custom-call | tf_op jit(solution)/shard_map/triangular_solve/custom-call.1 | solution.py:53
  1924.3 39.3 %custom-call.24 = f32[4,128,128]{1,2,0:T(8,128)S(1)} custom-call(f32[4,128,128]{2,1,0:T(8,128)S(1)} %get-tuple-element.110), custom_call_target="InvertDiagBlocksLowerTriangular" | custom-call | tf_op jit(solution)/shard_map/triangular_solve/custom-call.1 | solution.py:53
  2005.9 22.5 all_gather.308
  2038.3 39.3 %custom-call.31 = f32[4,128,128]{1,2,0:T(8,128)S(1)} custom-call(f32[4,128,128]{2,1,0:T(8,128)S(1)} %get-tuple-element.117), custom_call_target="InvertDiagBlocksLowerTriangular" | custom-call | tf_op jit(solution)/shard_map/triangular_solve/custom-call.1 | solution.py:53
  2089.1 39.3 %custom-call.30 = f32[4,128,128]{1,2,0:T(8,128)S(1)} custom-call(f32[4,128,128]{2,1,0:T(8,128)S(1)} %get-tuple-element.116), custom_call_target="InvertDiagBlocksLowerTriangular" | custom-call | tf_op jit(solution)/shard_map/triangular_solve/custom-call.1 | solution.py:53
  2139.4 39.3 %custom-call.33 = f32[4,128,128]{1,2,0:T(8,128)S(1)} custom-call(f32[4,128,128]{2,1,0:T(8,128)S(1)} %get-tuple-element.119), custom_call_target="InvertDiagBlocksLowerTriangular" | custom-call | tf_op jit(solution)/shard_map/triangular_solve/custom-call.1 | solution.py:53
  2192.2 40.7 %custom-call.26 = f32[4,128,128]{1,2,0:T(8,128)} custom-call(f32[4,128,128]{2,1,0:T(8,128)} %get-tuple-element.112), custom_call_target="InvertDiagBlocksLowerTriangular" | custom-call | tf_op jit(solution)/shard_map/triangular_solve/custom-call.1 | solution.py:53
  2238.4 12.9 all-gather.18
  2323.7 13.2 collective-permute-start.180
  2337.0 14.6 all_gather.338
  2352.0 12.8 all_gather.339
  2364.9 22.3 all_gather.336
  2398.3 26.3 all_gather.300
  2435.0 14.5 all-gather.11
  2521.3 14.6 all_gather.314
  2549.2 22.3 all_gather.312
  2606.1 39.3 %custom-call.32 = f32[4,128,128]{1,2,0:T(8,128)S(1)} custom-call(f32[4,128,128]{2,1,0:T(8,128)S(1)} %get-tuple-element.118), custom_call_target="InvertDiagBlocksLowerTriangular" | custom-call | tf_op jit(solution)/shard_map/triangular_solve/custom-call.1 | solution.py:53
  2648.8 14.9 all-gather.30
  2663.8 13.2 all-gather.26
  2703.6 22.6 all_gather.352
  2726.2 21.9 all_gather.344
  2803.7 14.6 all_gather.358
  2831.6 22.4 all_gather.356
  2975.2 53.6 %all-gather.111.cloned.1.call-done = f32[512,4096]{0,1:T(8,128)} async-done(((f32[512,256]{0,1:T(8,128)}), f32[512,4096]{0,1:T(8,128)}) %all-gather.111.cloned.1.call-update) | async-done | bytes 8388624 | tf_op jit(solution)/shard_map/all_gather | solution.py:41
  3028.7 17.0 fusion.435
  3059.0 67.7 %all-gather.109.cloned.1.call-done = f32[512,4096]{0,1:T(8,128)} async-done(((f32[512,256]{0,1:T(8,128)}), f32[512,4096]{0,1:T(8,128)}) %all-gather.109.cloned.1.call-update) | async-done | bytes 8388624 | tf_op jit(solution)/shard_map/all_gather | solution.py:41
  3126.7 37.2 %all-gather.115.cloned.1.call-done = f32[4096,256]{1,0:T(8,128)} async-done(((f32[512,256]{1,0:T(8,128)}), f32[4096,256]{1,0:T(8,128)}) %all-gather.115.cloned.1.call-update) | async-done | bytes 4194320 | tf_op jit(solution)/shard_map/all_gather | solution.py:42
  3208.0 20.3 collective-permute-done.299
  (1648 shorter events, 1705.0 us)
Async XLA Ops:
  6.5 822.6 %all-gather.67.cloned.1.call-start = ((), (), s32[]{:S(2)}) async-start(), calls=%async_computation.3 | async-start | bytes 1114112 | tf_op jit(solution)/shard_map/all_gather | solution.py:48
  139.4 769.9 %all-gather.65.cloned.1.call-start = ((), (), s32[]{:S(2)}) async-start(), calls=%async_computation.2 | async-start | bytes 1114112 | tf_op jit(solution)/shard_map/all_gather | solution.py:48
  169.7 821.5 %all-gather.63.cloned.1.call-start = ((), (), s32[]{:S(2)}) async-start(), calls=%async_computation.1 | async-start | bytes 1114112 | tf_op jit(solution)/shard_map/all_gather | solution.py:48
  206.5 840.7 %all-gather.61.cloned.1.call-start = ((), (), s32[]{:S(2)}) async-start(), calls=%async_computation | async-start | bytes 1114112 | tf_op jit(solution)/shard_map/all_gather | solution.py:48
  254.4 1262.6 %all-gather.91.cloned.1.call-start = ((), (), s32[]{:S(2)}) async-start(), calls=%async_computation.15 | async-start | bytes 1114112 | tf_op jit(solution)/shard_map/all_gather | solution.py:48
  300.9 1297.9 %all-gather.89.cloned.1.call-start = ((), (), s32[]{:S(2)}) async-start(), calls=%async_computation.14 | async-start | bytes 1114112 | tf_op jit(solution)/shard_map/all_gather | solution.py:48
  347.8 1334.8 %all-gather.87.cloned.1.call-start = ((), (), s32[]{:S(2)}) async-start(), calls=%async_computation.13 | async-start | bytes 1114112 | tf_op jit(solution)/shard_map/all_gather | solution.py:48
  388.3 1373.9 %all-gather.71.cloned.1.call-start = ((), (), s32[]{:S(2)}) async-start(), calls=%async_computation.5 | async-start | bytes 1114112 | tf_op jit(solution)/shard_map/all_gather | solution.py:48
  434.9 1379.3 %all-gather.69.cloned.1.call-start = ((), (), s32[]{:S(2)}) async-start(), calls=%async_computation.4 | async-start | bytes 1114112 | tf_op jit(solution)/shard_map/all_gather | solution.py:48
  466.1 1398.4 %all-gather.75.cloned.1.call-start = ((), (), s32[]{:S(2)}) async-start(), calls=%async_computation.7 | async-start | bytes 1114112 | tf_op jit(solution)/shard_map/all_gather | solution.py:48
  512.6 1402.1 %all-gather.73.cloned.1.call-start = ((), (), s32[]{:S(2)}) async-start(), calls=%async_computation.6 | async-start | bytes 1114112 | tf_op jit(solution)/shard_map/all_gather | solution.py:48
  555.1 1473.3 %all-gather.95.cloned.1.call-start = ((), (), s32[]{:S(2)}) async-start(), calls=%async_computation.17 | async-start | bytes 1114112 | tf_op jit(solution)/shard_map/all_gather | solution.py:48
  602.4 1477.1 %all-gather.93.cloned.1.call-start = ((), (), s32[]{:S(2)}) async-start(), calls=%async_computation.16 | async-start | bytes 1114112 | tf_op jit(solution)/shard_map/all_gather | solution.py:48
  632.8 1497.1 %all-gather.99.cloned.1.call-start = ((), (), s32[]{:S(2)}) async-start(), calls=%async_computation.19 | async-start | bytes 1114112 | tf_op jit(solution)/shard_map/all_gather | solution.py:48
  679.3 1500.6 %all-gather.85.cloned.1.call-start = ((), (), s32[]{:S(2)}) async-start(), calls=%async_computation.12 | async-start | bytes 1114112 | tf_op jit(solution)/shard_map/all_gather | solution.py:48
  709.8 1742.2 %all-gather.97.cloned.1.call-start = ((), (), s32[]{:S(2)}) async-start(), calls=%async_computation.18 | async-start | bytes 1114112 | tf_op jit(solution)/shard_map/all_gather | solution.py:48
  740.7 1744.9 %all-gather.79.cloned.1.call-start = ((), (), s32[]{:S(2)}) async-start(), calls=%async_computation.9 | async-start | bytes 2228224 | tf_op jit(solution)/shard_map/all_gather | solution.py:41
  749.7 1736.0 %all-gather.81.cloned.1.call-start = ((), (), s32[]{:S(2)}) async-start(), calls=%async_computation.10 | async-start | bytes 1179648 | tf_op jit(solution)/shard_map/all_gather | solution.py:42
  879.4 265.4 %collective-permute-start.56 = (f32[64,32]{0,1:T(8,128)S(1)}, f32[64,32]{0,1:T(8,128)S(1)}, u32[]{:S(2)}, u32[]{:S(2)}) collective-permute-start(f32[64,32]{0,1:T(8,128)S(1)} %fusion.295), channel_id=1, source_target_pairs={{0,64},{16,72},{32,80},{48,88},{64,96},{80,104},{96,112},{112,120}... | collective-permute-start | bytes 24584 | tf_op jit(solution)/shard_map/ppermute | solution.py:36
  884.6 260.9 %collective-permute-start.57 = (f32[64,32]{0,1:T(8,128)S(1)}, f32[64,32]{0,1:T(8,128)S(1)}, u32[]{:S(2)}, u32[]{:S(2)}) collective-permute-start(f32[64,32]{0,1:T(8,128)S(1)} %fusion.295), channel_id=1, source_target_pairs={{8,64},{24,72},{40,80},{56,88},{72,96},{88,104},{104,112},{120,120... | collective-permute-start | bytes 24584 | tf_op jit(solution)/shard_map/ppermute | solution.py:36
  985.3 161.5 %collective-permute-start.55 = (f32[64,32]{0,1:T(8,128)S(1)}, f32[64,32]{0,1:T(8,128)S(1)}, u32[]{:S(2)}, u32[]{:S(2)}) collective-permute-start(f32[64,32]{0,1:T(8,128)S(1)} %convolution_negate_fusion.13), channel_id=1, source_target_pairs={{8,0},{24,8},{40,16},{56,24},{72,32},{88,40},{104,48},{120,56},{9,... | collective-permute-start | bytes 24584 | tf_op jit(solution)/shard_map/ppermute | solution.py:36
  986.6 165.6 %collective-permute-start.54 = (f32[64,32]{0,1:T(8,128)S(1)}, f32[64,32]{0,1:T(8,128)S(1)}, u32[]{:S(2)}, u32[]{:S(2)}) collective-permute-start(f32[64,32]{0,1:T(8,128)S(1)} %convolution_negate_fusion.13), channel_id=1, source_target_pairs={{0,0},{16,8},{32,16},{48,24},{64,32},{80,40},{96,48},{112,56},{1,1... | collective-permute-start | bytes 24584 | tf_op jit(solution)/shard_map/ppermute | solution.py:36
  1041.7 129.4 %collective-permute-start.28 = (f32[64,32]{0,1:T(8,128)S(1)}, f32[64,32]{0,1:T(8,128)S(1)}, u32[]{:S(2)}, u32[]{:S(2)}) collective-permute-start(f32[64,32]{0,1:T(8,128)S(1)} %fusion.301), channel_id=1, source_target_pairs={{0,64},{16,72},{32,80},{48,88},{64,96},{80,104},{96,112},{112,120}... | collective-permute-start | bytes 24584 | tf_op jit(solution)/shard_map/ppermute | solution.py:36
  1188.4 75.8 %collective-permute-start.65 = (f32[128,64]{0,1:T(8,128)S(1)}, f32[128,64]{0,1:T(8,128)S(1)}, u32[]{:S(2)}, u32[]{:S(2)}) collective-permute-start(f32[128,64]{0,1:T(8,128)S(1)} %maximum_add_fusion.16), channel_id=1, source_target_pairs={{8,64},{24,72},{40,80},{56,88},{72,96},{88,104},{104,112},{120,120... | collective-permute-start | bytes 98312 | tf_op jit(solution)/shard_map/ppermute | solution.py:36
  1189.1 76.4 %collective-permute-start.64 = (f32[128,64]{0,1:T(8,128)S(1)}, f32[128,64]{0,1:T(8,128)S(1)}, u32[]{:S(2)}, u32[]{:S(2)}) collective-permute-start(f32[128,64]{0,1:T(8,128)S(1)} %maximum_add_fusion.16), channel_id=1, source_target_pairs={{0,64},{16,72},{32,80},{48,88},{64,96},{80,104},{96,112},{112,120}... | collective-permute-start | bytes 98312 | tf_op jit(solution)/shard_map/ppermute | solution.py:36
  1195.3 68.2 %collective-permute-start.33 = (f32[128,64]{0,1:T(8,128)S(1)}, f32[128,64]{0,1:T(8,128)S(1)}, u32[]{:S(2)}, u32[]{:S(2)}) collective-permute-start(f32[128,64]{0,1:T(8,128)S(1)} %maximum_add_fusion.14), channel_id=1, source_target_pairs={{8,0},{24,8},{40,16},{56,24},{72,32},{88,40},{104,48},{120,56},{9,... | collective-permute-start | bytes 98312 | tf_op jit(solution)/shard_map/ppermute | solution.py:36
  1196.7 63.1 %collective-permute-start.32 = (f32[128,64]{0,1:T(8,128)S(1)}, f32[128,64]{0,1:T(8,128)S(1)}, u32[]{:S(2)}, u32[]{:S(2)}) collective-permute-start(f32[128,64]{0,1:T(8,128)S(1)} %maximum_add_fusion.14), channel_id=1, source_target_pairs={{0,0},{16,8},{32,16},{48,24},{64,32},{80,40},{96,48},{112,56},{1,1... | collective-permute-start | bytes 98312 | tf_op jit(solution)/shard_map/ppermute | solution.py:36
  1274.3 1484.5 %all-gather.103.cloned.1.call-start = ((), (), s32[]{:S(2)}) async-start(), calls=%async_computation.21 | async-start | bytes 2228224 | tf_op jit(solution)/shard_map/all_gather | solution.py:41
  1285.1 1473.8 %all-gather.105.cloned.1.call-start = ((), (), s32[]{:S(2)}) async-start(), calls=%async_computation.22 | async-start | bytes 1179648 | tf_op jit(solution)/shard_map/all_gather | solution.py:42
  1370.5 78.4 %collective-permute-start.269 = (f32[64,32]{0,1:T(8,128)S(1)}, f32[64,32]{0,1:T(8,128)S(1)}, u32[]{:S(2)}, u32[]{:S(2)}) collective-permute-start(f32[64,32]{0,1:T(8,128)S(1)} %copy-done.76), channel_id=1, source_target_pairs={{4,1},{5,3},{6,5},{7,7},{12,9},{13,11},{14,13},{15,15},{20,17},{21... | collective-permute-start | bytes 24584 | tf_op jit(solution)/shard_map/ppermute | solution.py:22
  1371.9 79.0 %collective-permute-start.268 = (f32[64,32]{0,1:T(8,128)S(1)}, f32[64,32]{0,1:T(8,128)S(1)}, u32[]{:S(2)}, u32[]{:S(2)}) collective-permute-start(f32[64,32]{0,1:T(8,128)S(1)} %copy-done.74), channel_id=1, source_target_pairs={{4,0},{5,2},{6,4},{7,6},{12,8},{13,10},{14,12},{15,14},{20,16},{21... | collective-permute-start | bytes 24584 | tf_op jit(solution)/shard_map/ppermute | solution.py:22
  1399.9 95.4 %collective-permute-start.201 = (f32[64,32]{0,1:T(8,128)S(1)}, f32[64,32]{0,1:T(8,128)S(1)}, u32[]{:S(2)}, u32[]{:S(2)}) collective-permute-start(f32[64,32]{0,1:T(8,128)S(1)} %copy-done.56), channel_id=1, source_target_pairs={{4,1},{5,3},{6,5},{7,7},{12,9},{13,11},{14,13},{15,15},{20,17},{21... | collective-permute-start | bytes 24584 | tf_op jit(solution)/shard_map/ppermute | solution.py:22
  1422.8 72.5 %collective-permute-start.200 = (f32[64,32]{0,1:T(8,128)S(1)}, f32[64,32]{0,1:T(8,128)S(1)}, u32[]{:S(2)}, u32[]{:S(2)}) collective-permute-start(f32[64,32]{0,1:T(8,128)S(1)} %copy-done.54), channel_id=1, source_target_pairs={{4,0},{5,2},{6,4},{7,6},{12,8},{13,10},{14,12},{15,14},{20,16},{21... | collective-permute-start | bytes 24584 | tf_op jit(solution)/shard_map/ppermute | solution.py:22
  1568.5 705.8 %collective-permute-start.204 = (f32[64,32]{0,1:T(8,128)}, f32[64,32]{0,1:T(8,128)}, u32[]{:S(2)}, u32[]{:S(2)}) collective-permute-start(f32[64,32]{0,1:T(8,128)} %fusion.271), channel_id=1, source_target_pairs={{0,64},{16,72},{32,80},{48,88},{64,96},{80,104},{96,112},{112,120}... | collective-permute-start | bytes 24584 | tf_op jit(solution)/shard_map/ppermute | solution.py:36
  1574.2 700.8 %collective-permute-start.205 = (f32[64,32]{0,1:T(8,128)}, f32[64,32]{0,1:T(8,128)}, u32[]{:S(2)}, u32[]{:S(2)}) collective-permute-start(f32[64,32]{0,1:T(8,128)} %fusion.271), channel_id=1, source_target_pairs={{8,64},{24,72},{40,80},{56,88},{72,96},{88,104},{104,112},{120,120... | collective-permute-start | bytes 24584 | tf_op jit(solution)/shard_map/ppermute | solution.py:36
  1676.8 599.6 %collective-permute-start.203 = (f32[64,32]{0,1:T(8,128)}, f32[64,32]{0,1:T(8,128)}, u32[]{:S(2)}, u32[]{:S(2)}) collective-permute-start(f32[64,32]{0,1:T(8,128)} %convolution_negate_fusion.9), channel_id=1, source_target_pairs={{8,0},{24,8},{40,16},{56,24},{72,32},{88,40},{104,48},{120,56},{9,... | collective-permute-start | bytes 24584 | tf_op jit(solution)/shard_map/ppermute | solution.py:36
  1678.0 599.6 %collective-permute-start.202 = (f32[64,32]{0,1:T(8,128)}, f32[64,32]{0,1:T(8,128)}, u32[]{:S(2)}, u32[]{:S(2)}) collective-permute-start(f32[64,32]{0,1:T(8,128)} %convolution_negate_fusion.9), channel_id=1, source_target_pairs={{0,0},{16,8},{32,16},{48,24},{64,32},{80,40},{96,48},{112,56},{1,1... | collective-permute-start | bytes 24584 | tf_op jit(solution)/shard_map/ppermute | solution.py:36
  1733.7 558.1 %collective-permute-start.176 = (f32[64,32]{0,1:T(8,128)}, f32[64,32]{0,1:T(8,128)}, u32[]{:S(2)}, u32[]{:S(2)}) collective-permute-start(f32[64,32]{0,1:T(8,128)} %fusion.277), channel_id=1, source_target_pairs={{0,64},{16,72},{32,80},{48,88},{64,96},{80,104},{96,112},{112,120}... | collective-permute-start | bytes 24584 | tf_op jit(solution)/shard_map/ppermute | solution.py:36
  2296.7 175.9 %collective-permute-start.96 = (f32[64,32]{0,1:T(8,128)S(1)}, f32[64,32]{0,1:T(8,128)S(1)}, u32[]{:S(2)}, u32[]{:S(2)}) collective-permute-start(f32[64,32]{0,1:T(8,128)S(1)} %fusion.289), channel_id=1, source_target_pairs={{0,64},{16,72},{32,80},{48,88},{64,96},{80,104},{96,112},{112,120}... | collective-permute-start | bytes 24584 | tf_op jit(solution)/shard_map/ppermute | solution.py:36
  2317.4 75.2 %collective-permute-start.213 = (f32[128,64]{0,1:T(8,128)S(1)}, f32[128,64]{0,1:T(8,128)S(1)}, u32[]{:S(2)}, u32[]{:S(2)}) collective-permute-start(f32[128,64]{0,1:T(8,128)S(1)} %maximum_add_fusion.24), channel_id=1, source_target_pairs={{8,64},{24,72},{40,80},{56,88},{72,96},{88,104},{104,112},{120,120... | collective-permute-start | bytes 98312 | tf_op jit(solution)/shard_map/ppermute | solution.py:36
  2318.1 75.2 %collective-permute-start.212 = (f32[128,64]{0,1:T(8,128)S(1)}, f32[128,64]{0,1:T(8,128)S(1)}, u32[]{:S(2)}, u32[]{:S(2)}) collective-permute-start(f32[128,64]{0,1:T(8,128)S(1)} %maximum_add_fusion.24), channel_id=1, source_target_pairs={{0,64},{16,72},{32,80},{48,88},{64,96},{80,104},{96,112},{112,120}... | collective-permute-start | bytes 98312 | tf_op jit(solution)/shard_map/ppermute | solution.py:36
  2322.4 66.5 %collective-permute-start.181 = (f32[128,64]{0,1:T(8,128)S(1)}, f32[128,64]{0,1:T(8,128)S(1)}, u32[]{:S(2)}, u32[]{:S(2)}) collective-permute-start(f32[128,64]{0,1:T(8,128)S(1)} %maximum_add_fusion.22), channel_id=1, source_target_pairs={{8,0},{24,8},{40,16},{56,24},{72,32},{88,40},{104,48},{120,56},{9,... | collective-permute-start | bytes 98312 | tf_op jit(solution)/shard_map/ppermute | solution.py:36
  2323.7 63.9 %collective-permute-start.180 = (f32[128,64]{0,1:T(8,128)S(1)}, f32[128,64]{0,1:T(8,128)S(1)}, u32[]{:S(2)}, u32[]{:S(2)}) collective-permute-start(f32[128,64]{0,1:T(8,128)S(1)} %maximum_add_fusion.22), channel_id=1, source_target_pairs={{0,0},{16,8},{32,16},{48,24},{64,32},{80,40},{96,48},{112,56},{1,1... | collective-permute-start | bytes 98312 | tf_op jit(solution)/shard_map/ppermute | solution.py:36
  2435.0 449.8 %all-gather.83.cloned.1.call-start = ((), (), s32[]{:S(2)}) async-start(), calls=%async_computation.11 | async-start | bytes 1179648 | tf_op jit(solution)/shard_map/all_gather | solution.py:42
  2475.3 278.9 %collective-permute-start.272 = (f32[64,32]{0,1:T(8,128)S(1)}, f32[64,32]{0,1:T(8,128)S(1)}, u32[]{:S(2)}, u32[]{:S(2)}) collective-permute-start(f32[64,32]{0,1:T(8,128)S(1)} %fusion.259), channel_id=1, source_target_pairs={{0,64},{16,72},{32,80},{48,88},{64,96},{80,104},{96,112},{112,120}... | collective-permute-start | bytes 24584 | tf_op jit(solution)/shard_map/ppermute | solution.py:36
  2491.6 393.1 %all-gather.77.cloned.1.call-start = ((), (), s32[]{:S(2)}) async-start(), calls=%async_computation.8 | async-start | bytes 2228224 | tf_op jit(solution)/shard_map/all_gather | solution.py:41
  2504.4 72.5 %collective-permute-start.133 = (f32[128,64]{0,1:T(8,128)S(1)}, f32[128,64]{0,1:T(8,128)S(1)}, u32[]{:S(2)}, u32[]{:S(2)}) collective-permute-start(f32[128,64]{0,1:T(8,128)S(1)} %maximum_add_fusion.20), channel_id=1, source_target_pairs={{8,64},{24,72},{40,80},{56,88},{72,96},{88,104},{104,112},{120,120... | collective-permute-start | bytes 98312 | tf_op jit(solution)/shard_map/ppermute | solution.py:36
  2505.1 72.5 %collective-permute-start.132 = (f32[128,64]{0,1:T(8,128)S(1)}, f32[128,64]{0,1:T(8,128)S(1)}, u32[]{:S(2)}, u32[]{:S(2)}) collective-permute-start(f32[128,64]{0,1:T(8,128)S(1)} %maximum_add_fusion.20), channel_id=1, source_target_pairs={{0,64},{16,72},{32,80},{48,88},{64,96},{80,104},{96,112},{112,120}... | collective-permute-start | bytes 98312 | tf_op jit(solution)/shard_map/ppermute | solution.py:36
  2582.4 172.4 %collective-permute-start.273 = (f32[64,32]{0,1:T(8,128)S(1)}, f32[64,32]{0,1:T(8,128)S(1)}, u32[]{:S(2)}, u32[]{:S(2)}) collective-permute-start(f32[64,32]{0,1:T(8,128)S(1)} %fusion.259), channel_id=1, source_target_pairs={{8,64},{24,72},{40,80},{56,88},{72,96},{88,104},{104,112},{120,120... | collective-permute-start | bytes 24584 | tf_op jit(solution)/shard_map/ppermute | solution.py:36
  2583.1 187.8 %collective-permute-start.244 = (f32[64,32]{0,1:T(8,128)S(1)}, f32[64,32]{0,1:T(8,128)S(1)}, u32[]{:S(2)}, u32[]{:S(2)}) collective-permute-start(f32[64,32]{0,1:T(8,128)S(1)} %fusion.265), channel_id=1, source_target_pairs={{0,64},{16,72},{32,80},{48,88},{64,96},{80,104},{96,112},{112,120}... | collective-permute-start | bytes 24584 | tf_op jit(solution)/shard_map/ppermute | solution.py:36
  2589.1 159.6 %collective-permute-start.232 = (f32[64,32]{0,1:T(8,128)S(1)}, f32[64,32]{0,1:T(8,128)S(1)}, u32[]{:S(2)}, u32[]{:S(2)}) collective-permute-start(f32[64,32]{0,1:T(8,128)S(1)} %fusion.268), channel_id=1, source_target_pairs={{0,0},{16,8},{32,16},{48,24},{64,32},{80,40},{96,48},{112,56},{1,1... | collective-permute-start | bytes 24584 | tf_op jit(solution)/shard_map/ppermute | solution.py:36
  2597.1 352.9 %all-gather.107.cloned.1.call-start = ((), (), s32[]{:S(2)}) async-start(), calls=%async_computation.23 | async-start | bytes 1179648 | tf_op jit(solution)/shard_map/all_gather | solution.py:42
  2646.8 103.1 %collective-permute-start.260 = (f32[64,32]{0,1:T(8,128)S(1)}, f32[64,32]{0,1:T(8,128)S(1)}, u32[]{:S(2)}, u32[]{:S(2)}) collective-permute-start(f32[64,32]{0,1:T(8,128)S(1)} %fusion.262), channel_id=1, source_target_pairs={{0,0},{16,8},{32,16},{48,24},{64,32},{80,40},{96,48},{112,56},{1,1... | collective-permute-start | bytes 24584 | tf_op jit(solution)/shard_map/ppermute | solution.py:36
  2764.9 185.2 %all-gather.101.cloned.1.call-start = ((), (), s32[]{:S(2)}) async-start(), calls=%async_computation.20 | async-start | bytes 2228224 | tf_op jit(solution)/shard_map/all_gather | solution.py:41
  2788.3 72.6 %collective-permute-start.281 = (f32[128,64]{0,1:T(8,128)S(1)}, f32[128,64]{0,1:T(8,128)S(1)}, u32[]{:S(2)}, u32[]{:S(2)}) collective-permute-start(f32[128,64]{0,1:T(8,128)S(1)} %maximum_add_fusion.28), channel_id=1, source_target_pairs={{8,64},{24,72},{40,80},{56,88},{72,96},{88,104},{104,112},{120,120... | collective-permute-start | bytes 98312 | tf_op jit(solution)/shard_map/ppermute | solution.py:36
  2789.0 73.2 %collective-permute-start.280 = (f32[128,64]{0,1:T(8,128)S(1)}, f32[128,64]{0,1:T(8,128)S(1)}, u32[]{:S(2)}, u32[]{:S(2)}) collective-permute-start(f32[128,64]{0,1:T(8,128)S(1)} %maximum_add_fusion.28), channel_id=1, source_target_pairs={{0,64},{16,72},{32,80},{48,88},{64,96},{80,104},{96,112},{112,120}... | collective-permute-start | bytes 98312 | tf_op jit(solution)/shard_map/ppermute | solution.py:36
  2871.1 104.1 %all-gather.113.cloned.1.call-start = ((), (), s32[]{:S(2)}) async-start(), calls=%async_computation.26 | async-start | bytes 4718592 | tf_op jit(solution)/shard_map/all_gather | solution.py:42
  2912.9 115.9 %all-gather.111.cloned.1.call-start = ((), (), s32[]{:S(2)}) async-start(), calls=%async_computation.25 | async-start | bytes 8912896 | tf_op jit(solution)/shard_map/all_gather | solution.py:41
  2935.2 191.5 %all-gather.109.cloned.1.call-start = ((), (), s32[]{:S(2)}) async-start(), calls=%async_computation.24 | async-start | bytes 8912896 | tf_op jit(solution)/shard_map/all_gather | solution.py:41
  2974.9 189.0 %all-gather.115.cloned.1.call-start = ((), (), s32[]{:S(2)}) async-start(), calls=%async_computation.27 | async-start | bytes 4718592 | tf_op jit(solution)/shard_map/all_gather | solution.py:42
  3045.8 135.0 %collective-permute-start.145 = (f32[512,256]{0,1:T(8,128)S(1)}, f32[512,256]{0,1:T(8,128)S(1)}, u32[]{:S(2)}, u32[]{:S(2)}) collective-permute-start(f32[512,256]{0,1:T(8,128)S(1)} %copy-done.2), channel_id=1, source_target_pairs={{8,0},{24,8},{40,16},{56,24},{72,32},{88,40},{104,48},{120,56},{9,... | collective-permute-start | bytes 1572872 | tf_op jit(solution)/shard_map/ppermute | solution.py:36
  3047.1 128.8 %collective-permute-start.144 = (f32[512,256]{0,1:T(8,128)S(1)}, f32[512,256]{0,1:T(8,128)S(1)}, u32[]{:S(2)}, u32[]{:S(2)}) collective-permute-start(f32[512,256]{0,1:T(8,128)S(1)} %copy-done.2), channel_id=1, source_target_pairs={{0,0},{16,8},{32,16},{48,24},{64,32},{80,40},{96,48},{112,56},{1,1... | collective-permute-start | bytes 1572872 | tf_op jit(solution)/shard_map/ppermute | solution.py:36
  3052.2 129.5 %collective-permute-start.297 = (f32[512,256]{0,1:T(8,128)S(1)}, f32[512,256]{0,1:T(8,128)S(1)}, u32[]{:S(2)}, u32[]{:S(2)}) collective-permute-start(f32[512,256]{0,1:T(8,128)S(1)} %copy-done.3), channel_id=1, source_target_pairs={{8,64},{24,72},{40,80},{56,88},{72,96},{88,104},{104,112},{120,120... | collective-permute-start | bytes 1572872 | tf_op jit(solution)/shard_map/ppermute | solution.py:36
  3052.9 135.1 %collective-permute-start.296 = (f32[512,256]{0,1:T(8,128)S(1)}, f32[512,256]{0,1:T(8,128)S(1)}, u32[]{:S(2)}, u32[]{:S(2)}) collective-permute-start(f32[512,256]{0,1:T(8,128)S(1)} %copy-done.3), channel_id=1, source_target_pairs={{0,64},{16,72},{32,80},{48,88},{64,96},{80,104},{96,112},{112,120}... | collective-permute-start | bytes 1572872 | tf_op jit(solution)/shard_map/ppermute | solution.py:36
  (341 other events, 8874.8 us)
Sparse Core Ops, SparseCore 0:
  139.5 51.8 all-gather.66
  193.6 45.0 all-gather.64
  240.8 41.7 all-gather.62
  284.7 42.2 all-gather.60
  328.9 41.1 all-gather.90
  372.1 43.1 all-gather.88
  417.4 41.6 all-gather.86
  461.3 41.8 all-gather.70
  505.3 42.3 all-gather.68
  549.6 42.6 all-gather.74
  594.5 42.0 all-gather.72
  638.5 41.6 all-gather.94
  682.3 41.6 all-gather.92
  726.0 41.6 all-gather.98
  769.7 42.4 all-gather.84
  814.2 41.7 all-gather.96
  858.0 44.8 all-gather.78
  1274.4 26.3 all-gather.80
  1302.9 46.4 all-gather.102
  2435.1 26.1 all-gather.104
  2491.7 22.4 all-gather.82
  2597.2 44.8 all-gather.76
  2765.0 30.6 all-gather.106
  2871.2 51.3 all-gather.100
  2924.3 29.5 all-gather.112
  2955.9 72.7 all-gather.110
  3030.7 95.8 all-gather.108
  3128.4 35.4 all-gather.114
where the time goes:
time: 3280 us; the launch traced here: 3240 us
  blocking collectives  1080 us (33%)
  starting transfers between devices  693 us (21%)
  other arithmetic  666 us (20%)
  waiting for transfers between devices  524 us (16%)
  local copies, waits for them, and re-layouts  166 us (5%)
  matrix products  90.4 us (3%)
    another operation x49, other arithmetic, leaf_inverse(): lax.linalg.triangular_solve(leaf_mat, eye_cols, left_side=True, lower=True)  655 us
    all_gather x24, blocking collectives, summa_prod(): left_rows = lax.all_gather(left_tile, 'col', axis=1, tiled=True)  545 us
    ppermute x150, starting transfers between devices, put_half(): slot_list.append(lax.ppermute(local_tile, axis_name, pair_list))  416 us
    all_gather x24, blocking collectives, summa_prod(): right_cols = lax.all_gather(right_tile, 'row', axis=0, tiled=True)  318 us
    ppermute x150, waiting for transfers between devices, take_half(): received.append(lax.ppermute(halves[half_idx], axis_name, pair_list))  296 us
    ppermute x150, starting transfers between devices, take_half(): received.append(lax.ppermute(halves[half_idx], axis_name, pair_list))  276 us
    all_gather x16, blocking collectives, leaf_inverse(): row_panel = lax.all_gather(local_tile, 'row', axis=0, tiled=True)  213 us
    another operation x336, local copies, waits for them, and re-layouts, leaf_inverse(): lax.linalg.triangular_solve(leaf_mat, eye_cols, left_side=True, lower=True)  134 us
  transfers between devices with their start and end apart: 328, of which 87 were waited for; matrix products, arithmetic and copies ran while one was open for 28% of the time, Pallas kernels for 0%

commit v1 on v0

v1 whole, which is shorter than its diff:
```python
import jax
import jax.numpy as jnp
from jax import lax
from jax.experimental import pallas as pl
from jax.experimental.pallas import tpu as pltpu
from jax.sharding import Mesh, PartitionSpec as P

F32 = jnp.float32
AXES = ("z", "y", "x", "core")
NZ, NY, NX, NK = 4, 4, 4, 2
COORDS = [(z, y, x, k) for z in range(NZ) for y in range(NY) for x in range(NX) for k in range(NK)]
INDEX = {c: i for i, c in enumerate(COORDS)}
LEAF, BASE, SUB = 512, 128, 128


def dot(left, right):
    return jnp.dot(left, right, precision=lax.Precision.HIGHEST, preferred_element_type=F32)


def dot_blocks(left, right):
    return lax.dot_general(left, right, (((0, 2), (0, 1)), ((), ())), precision=lax.Precision.HIGHEST, preferred_element_type=F32)


def leaf_kernel(m_ref, o_ref):
    rows = lax.broadcasted_iota(jnp.int32, (BASE, BASE), 0)
    cols = lax.broadcasted_iota(jnp.int32, (BASE, BASE), 1)
    eye = (rows == cols).astype(F32)
    o_ref[...] = jnp.zeros_like(o_ref)
    powers, sums, recips = [], [], []
    for b in range(LEAF // BASE):
        s = slice(b * BASE, (b + 1) * BASE)
        blk = m_ref[s, s]
        diag = jnp.where(rows == cols, blk, 0.0)
        recip_col = 1.0 / jnp.sum(diag, axis=1, keepdims=True)
        recips.append(1.0 / jnp.sum(diag, axis=0, keepdims=True))
        strict = jnp.where(rows > cols, blk, 0.0) * recip_col
        sums.append(eye - strict)
        powers.append(dot(strict, strict))
    steps = BASE.bit_length() - 2
    for i in range(steps):
        sums = [p + dot(p, q) for p, q in zip(sums, powers)]
        if i < steps - 1:
            powers = [dot(q, q) for q in powers]
    for b in range(LEAF // BASE):
        s = slice(b * BASE, (b + 1) * BASE)
        o_ref[s, s] = sums[b] * recips[b]
    size = BASE
    while size < LEAF:
        prods = []
        for lo in range(0, LEAF, 2 * size):
            a, c = slice(lo, lo + size), slice(lo + size, lo + 2 * size)
            prods.append((a, c, dot(m_ref[c, a], o_ref[a, a])))
        for a, c, t in prods:
            o_ref[c, a] = -dot(o_ref[c, c], t)
        size *= 2


def leaf_inverse(half):
    return pl.pallas_call(
        leaf_kernel,
        out_shape=jax.ShapeDtypeStruct((LEAF, LEAF), F32),
        in_specs=[pl.BlockSpec(memory_space=pltpu.VMEM)],
        out_specs=pl.BlockSpec(memory_space=pltpu.VMEM),
        cost_estimate=pl.CostEstimate(flops=20_000_000, bytes_accessed=2_000_000, transcendentals=0),
    )(half)


def route(tile, rule):
    pairs = []
    for c in COORDS:
        dest = rule(*c)
        if dest is not None:
            pairs.append((INDEX[c], INDEX[dest]))
    return lax.ppermute(tile, AXES, pairs)


def invert(t):
    z, y, x, k = (lax.axis_index(a) for a in AXES)
    on_diag = z == x
    leaf0 = on_diag & (y == 2 * k)
    leaf1 = on_diag & (y == 2 * k + 1)
    x_odd = x % 2 == 1

    c3 = jnp.zeros((LEAF, SUB), F32)
    for h in range(2):
        for q in range(4):
            piece = t[h * LEAF:(h + 1) * LEAF, q * SUB:(q + 1) * SUB]
            c3 = c3 + route(piece, lambda zz, yy, xx, kk, h=h, q=q: (q, yy, xx - h, kk) if xx % 2 == 1 and zz == xx - 1 else None)
    g3 = lax.all_gather(c3, ("z", "y"), axis=0)
    c4 = jnp.zeros((LEAF, 2 * SUB), F32)
    for h in range(2):
        for p in range(2):
            piece = t[h * LEAF:(h + 1) * LEAF, p * 2 * SUB:(p + 1) * 2 * SUB]
            c4 = c4 + route(piece, lambda zz, yy, xx, kk, h=h, p=p: (3 - zz if p else zz, yy, 3 - xx if h else xx, kk) if xx >= 2 and zz < 2 else None)
    g4 = lax.all_gather(c4, ("z", "y"), axis=0)

    rows = lax.broadcasted_iota(jnp.int32, (LEAF, LEAF), 0)
    cols = lax.broadcasted_iota(jnp.int32, (LEAF, LEAF), 1)
    eye = (rows == cols).astype(F32)
    half = jnp.where(leaf0, t[:LEAF], jnp.where(leaf1, t[LEAF:], eye))
    inv = leaf_inverse(half)

    inv_next = route(inv, lambda zz, yy, xx, kk: (zz, yy - 1, xx, kk) if zz == xx and yy == 2 * kk + 1 else None)
    x10 = -dot(inv_next, dot(t[LEAF:], inv))
    zero = jnp.zeros((LEAF, LEAF), F32)
    ecol = jnp.concatenate([jnp.where(leaf0, inv, zero), jnp.where(leaf0, x10, jnp.where(leaf1, inv, zero))], axis=0)

    c_other = route(t, lambda zz, yy, xx, kk: (zz, 1 - yy, xx, kk) if zz == xx and yy < 2 and kk == 1 else None)
    first, second = jnp.where(y == 0, t, c_other), jnp.where(y == 0, c_other, t)
    acol = route(ecol, lambda zz, yy, xx, kk: (zz, yy, xx, 1) if zz == xx and yy < 2 and kk == 0 else None)
    t2 = dot(first, acol[:LEAF]) + dot(second, acol[LEAF:])
    near = route(inv, lambda zz, yy, xx, kk: (zz, {2: 1, 3: 0}[yy], xx, kk) if zz == xx and yy >= 2 and kk == 1 else None)
    far = route(inv, lambda zz, yy, xx, kk: (zz, {2: 0, 3: 1}[yy], xx, kk) if zz == xx and yy >= 2 and kk == 1 else None)
    inv2 = jnp.where(y == 0, far, near)
    inv3 = jnp.where(y == 0, near, far)
    x32 = route(x10, lambda zz, yy, xx, kk: (zz, 1, xx, kk) if zz == xx and yy == 2 and kk == 1 else None) \
        + route(x10, lambda zz, yy, xx, kk: (zz, 0, xx, kk) if zz == xx and yy == 2 and kk == 1 else None)
    top = dot(inv2, t2[:LEAF])
    bot = dot(x32, t2[:LEAF]) + dot(inv3, t2[LEAF:])
    low = jnp.concatenate([-top, -bot], axis=0)
    dg = jnp.where(on_diag & (k == 1) & (y < 2), low, ecol)

    dq = jnp.zeros((2 * LEAF, SUB), F32)
    for q in range(4):
        dq = dq + route(dg[:, q * SUB:(q + 1) * SUB], lambda zz, yy, xx, kk, q=q: (q, yy, xx, kk) if zz == xx else None)

    def by_zy(mat):
        return mat.reshape(4, 4, SUB, mat.shape[1]).transpose(1, 0, 2, 3).reshape(16, SUB, mat.shape[1])

    lower = dq[LEAF:]
    d3 = jnp.where(x_odd, dq[:LEAF], route(lower, lambda zz, yy, xx, kk: (zz, yy, xx - 1, kk) if xx % 2 == 1 else None))
    gd3 = lax.all_gather(d3, ("z", "y"), axis=0)
    d_flip = route(dq, lambda zz, yy, xx, kk: (zz, yy, xx, 1 - kk) if xx % 2 == 0 else None)
    d_hop = route(dq, lambda zz, yy, xx, kk: (zz, yy, xx + 1, kk) if xx % 2 == 0 else None)
    d_both = route(dq, lambda zz, yy, xx, kk: (zz, yy, xx + 1, 1 - kk) if xx % 2 == 0 else None)
    own = jnp.where(x_odd, d_hop, dq)
    other = jnp.where(x_odd, d_both, d_flip)
    ds = jnp.concatenate([jnp.where(k == 0, own, other), jnp.where(k == 0, other, own)], axis=0)
    t3 = dot_blocks(g3, by_zy(ds))
    t3_k = route(t3, lambda zz, yy, xx, kk: (zz, yy, xx, 1 - kk))
    t3_x = route(t3, lambda zz, yy, xx, kk: (zz, yy, xx ^ 1, kk))
    t3_xk = route(t3, lambda zz, yy, xx, kk: (zz, yy, xx ^ 1, 1 - kk))

    def part(odd, core):
        same_x = x_odd if odd else jnp.logical_not(x_odd)
        same_k = k == core
        return jnp.where(same_x, jnp.where(same_k, t3, t3_k), jnp.where(same_k, t3_x, t3_xk))

    t3_full = jnp.concatenate([part(True, 0), part(False, 0), part(True, 1), part(False, 1)], axis=0)
    x3 = -dot_blocks(gd3, by_zy(t3_full))

    team_d = lax.all_gather(dq, ("x", "core"), axis=0)
    team_x = lax.all_gather(x3, ("x", "core"), axis=0)
    d0 = team_d[0:2].reshape(2048, SUB)
    d1 = team_d[2:4].reshape(2048, SUB)
    x10s = jnp.concatenate([team_x[2], team_x[0], team_x[3], team_x[1]], axis=0)
    a_top = jnp.concatenate([d0, jnp.zeros_like(d0)], axis=1)
    a_bot = jnp.concatenate([x10s, d1], axis=1)
    a_mat = jnp.concatenate([a_top, a_bot], axis=0).reshape(2, 4, 2, 2 * SUB, 2 * SUB)
    a_blocks = jnp.stack([a_mat[0, :, 0], a_mat[1, :, 0], a_mat[1, :, 1], a_mat[0, :, 1]]).reshape(16, 2 * SUB, 2 * SUB)
    t4 = dot_blocks(g4, a_blocks)
    inner = (x == 1) | (x == 2)
    dt = jnp.where(x >= 2, dq[:LEAF], route(lower, lambda zz, yy, xx, kk: (zz, yy, 3 - xx, kk) if xx >= 2 else None))
    xt = jnp.where(x == 3, x3, route(x3, lambda zz, yy, xx, kk: (zz, yy, 0, kk) if xx == 2 else None))
    g_second = lax.all_gather(jnp.where(inner, 0.0, dt), ("z", "y"), axis=0)
    g_first = lax.all_gather(jnp.where(inner, dt, xt), ("z", "y"), axis=0)
    team_t = lax.all_gather(t4, ("x", "core"), axis=0)
    t_first = jnp.concatenate([team_t[4], team_t[2], team_t[5], team_t[3]], axis=0)
    t_second = jnp.concatenate([team_t[6], team_t[0], team_t[7], team_t[1]], axis=0)
    x4 = -(dot_blocks(g_first, by_zy(t_first)) + dot_blocks(g_second, by_zy(t_second)))

    out = dg
    pieces = []
    for h in range(2):
        row = []
        for q in range(4):
            got = route(x3, lambda zz, yy, xx, kk, h=h, q=q: (xx | 1) - 1 >= 0 and (((xx | 1) - 1), yy, xx | 1, kk) if zz == q and (xx % 2 == 1) == (h == 0) else None)
            for j in range(2):
                got = got + route(x4[:, j * SUB:(j + 1) * SUB], lambda zz, yy, xx, kk, h=h, q=q, j=j: (j, yy, xx if h == 0 else 3 - xx, kk) if zz == q and (xx >= 2) == (h == 0) else None)
            row.append(got)
        pieces.append(jnp.concatenate(row, axis=1))
    return out + jnp.concatenate(pieces, axis=0)


def solution(mesh):
    grid = Mesh(mesh.devices.reshape(NZ, NY, NX, NK), AXES)
    spec = P(("x", "core"), ("z", "y"))
    return jax.shard_map(invert, mesh=grid, in_specs=(spec,), out_specs=spec, check_vma=False)
```

time: 3280 us -> 671 us (0.20)
  blocking collectives: 1080 us -> 0 us
  other arithmetic: 666 us -> 17.9 us
  starting transfers between devices: 693 us -> 312 us
  waiting for transfers between devices: 524 us -> 240 us
  local copies, waits for them, and re-layouts: 166 us -> 11.3 us
    all_gather x64 -> x0, blocking collectives: 1080 us -> none  [the longest x24 545 us: summa_prod(): left_rows = lax.all_gather(left_tile, 'col', axis=1, tiled=True)]
    another operation x49 -> x1, other arithmetic: 655 us -> 2.45 us  [invert(): jnp.stack([a_mat[0, :, 0], a_mat[1, :, 0], a_mat[1, :, 1], a_mat[0, :, 1]])]
    ppermute x300 -> x56, starting transfers between devices: 691 us -> 312 us  [route(): return lax.ppermute(tile, AXES, pairs)]
    ppermute x300 -> x56, waiting for transfers between devices: 365 us -> 85.8 us  [route(): return lax.ppermute(tile, AXES, pairs)]
    another operation x336 -> x1, local copies, waits for them, and re-layouts: 134 us -> 0.41 us  [invert(): jnp.stack([a_mat[0, :, 0], a_mat[1, :, 0], a_mat[1, :, 1], a_mat[0, :, 1]])]
    all_gather x28 -> x8, waiting for transfers between devices: 159 us -> 153 us  [the longest x1 62.6 us: invert(): g4 = lax.all_gather(c4, ('z', 'y'), axis=0)]
  transfers between devices with their start and end apart: 328 -> 64, of which waited for: 87 -> 17; matrix products, arithmetic and copies ran while one was open for 28% -> 11% of each run, Pallas kernels for 0% -> 1%
where the time goes in v1:
time: 671 us; the launch traced here: 662 us
  starting transfers between devices  312 us (46%)
  waiting for transfers between devices  240 us (36%)
  matrix products  59 us (9%)
  other arithmetic  17.9 us (3%)
  between operations  15 us (2%)
  local copies, waits for them, and re-layouts  11.3 us (2%)
    ppermute x56, starting transfers between devices, route(): return lax.ppermute(tile, AXES, pairs)  312 us
    ppermute x56, waiting for transfers between devices, route(): return lax.ppermute(tile, AXES, pairs)  85.8 us
    all_gather x1, waiting for transfers between devices, invert(): g4 = lax.all_gather(c4, ('z', 'y'), axis=0)  62.6 us
    all_gather x1, waiting for transfers between devices, invert(): g_first = lax.all_gather(jnp.where(inner, dt, xt), ('z', 'y'), axis=0)  47.4 us
    all_gather x1, waiting for transfers between devices, invert(): g_second = lax.all_gather(jnp.where(inner, 0.0, dt), ('z', 'y'), axis=0)  42.8 us
    dot_general x5, matrix products, dot_blocks(): lax.dot_general(left, right, (((0, 2), (0, 1)), ((), ())), precision=lax....  33.1 us
    dot_general x7, matrix products, dot(): jnp.dot(left, right, precision=lax.Precision.HIGHEST, preferred_element_t...  25.9 us
  transfers between devices with their start and end apart: 64, of which 17 were waited for; matrix products, arithmetic and copies ran while one was open for 11% of the time, Pallas kernels for 1%

profile of v1, /device:TPU:38, one launch (start us, length us, event | category | flops | bytes accessed | tf_op | source)
XLA Modules:
  0.0 662.1 jit_solution(9768578711543233949)
XLA Ops:
  6.5 1.7 fusion.29
  9.1 1.3 collective-permute-start.13
  13.1 6.1 collective-permute-done.13
  22.7 6.6 shard_map.17
  30.1 2.0 collective-permute-start.2
  32.1 4.7 fusion.22
  36.9 3.0 broadcast_select_fusion
  39.8 1.6 pad_maximum_fusion.1
  41.9 2.0 collective-permute-start.4
  43.9 1.7 collective-permute-start
  45.6 1.6 collective-permute-start.1
  49.1 5.3 fusion
  54.5 4.7 fusion.4
  59.2 3.1 convolution_negate_fusion
  62.3 3.1 fusion.11
  65.5 1.9 fusion.7
  69.4 70.3 %collective-permute-start.10 = (f32[1024,128]{1,0:T(8,128)S(1)}, f32[1024,128]{1,0:T(8,128)S(1)}, u32[]{:S(2)}, u32[]{:S(2)}) collective-permute-start(f32[1024,128]{1,0:T(8,128)S(1)} %get-tuple-element.38), channel_id=1, source_target_pairs={{0,96},{1,97},{8,104},{9,105},{16,112},{17,113},{24,120},{25,121},... | collective-permute-start | bytes 1572872 | tf_op jit(solution)/shard_map/ppermute | solution.py:74
  139.8 10.2 %collective-permute-start.7 = (f32[1024,128]{1,0:T(8,128)S(1)}, f32[1024,128]{1,0:T(8,128)S(1)}, u32[]{:S(2)}, u32[]{:S(2)}) collective-permute-start(f32[1024,128]{1,0:T(8,128)S(1)} %get-tuple-element.40), channel_id=1, source_target_pairs={{0,0},{1,1},{8,8},{9,9},{16,16},{17,17},{24,24},{25,25},{34,2},{35... | collective-permute-start | bytes 1572872 | tf_op jit(solution)/shard_map/ppermute | solution.py:74
  150.0 10.2 %collective-permute-start.8 = (f32[1024,128]{1,0:T(8,128)S(1)}, f32[1024,128]{1,0:T(8,128)S(1)}, u32[]{:S(2)}, u32[]{:S(2)}) collective-permute-start(f32[1024,128]{1,0:T(8,128)S(1)} %get-tuple-element.37), channel_id=1, source_target_pairs={{0,32},{1,33},{8,40},{9,41},{16,48},{17,49},{24,56},{25,57},{34,34... | collective-permute-start | bytes 1572872 | tf_op jit(solution)/shard_map/ppermute | solution.py:74
  160.2 10.2 %collective-permute-start.9 = (f32[1024,128]{1,0:T(8,128)S(1)}, f32[1024,128]{1,0:T(8,128)S(1)}, u32[]{:S(2)}, u32[]{:S(2)}) collective-permute-start(f32[1024,128]{1,0:T(8,128)S(1)} %get-tuple-element.39), channel_id=1, source_target_pairs={{0,64},{1,65},{8,72},{9,73},{16,80},{17,81},{24,88},{25,89},{34,66... | collective-permute-start | bytes 1572872 | tf_op jit(solution)/shard_map/ppermute | solution.py:74
  170.4 5.8 collective-permute-done.8
  176.3 19.4 %collective-permute-start.11 = (f32[512,128]{1,0:T(8,128)S(1)}, f32[512,128]{1,0:T(8,128)S(1)}, u32[]{:S(2)}, u32[]{:S(2)}) collective-permute-start(f32[512,128]{1,0:T(8,128)S(1)} %slice.216), channel_id=1, source_target_pairs={{2,0},{3,1},{6,4},{7,5},{10,8},{11,9},{14,12},{15,13},{18,16},{19,... | collective-permute-start | bytes 786440 | tf_op jit(solution)/shard_map/ppermute | solution.py:74
  195.7 6.1 collective-permute-done.11
  203.4 11.2 %collective-permute-start.20 = (f32[1024,128]{1,0:T(8,128)}, f32[1024,128]{1,0:T(8,128)S(1)}, u32[]{:S(2)}, u32[]{:S(2)}) collective-permute-start(f32[1024,128]{1,0:T(8,128)} %copy-done.3), channel_id=1, source_target_pairs={{0,2},{1,3},{4,6},{5,7},{8,10},{9,11},{12,14},{13,15},{16,18},{17,... | collective-permute-start | bytes 1572872 | tf_op jit(solution)/shard_map/ppermute | solution.py:74
  214.6 10.2 %collective-permute-start.21 = (f32[1024,128]{1,0:T(8,128)}, f32[1024,128]{1,0:T(8,128)S(1)}, u32[]{:S(2)}, u32[]{:S(2)}) collective-permute-start(f32[1024,128]{1,0:T(8,128)} %copy-done.3), channel_id=1, source_target_pairs={{0,3},{1,2},{4,7},{5,6},{8,11},{9,10},{12,15},{13,14},{16,19},{17,... | collective-permute-start | bytes 1572872 | tf_op jit(solution)/shard_map/ppermute | solution.py:74
  224.8 11.0 %collective-permute-start.22 = (f32[1024,128]{1,0:T(8,128)}, f32[1024,128]{1,0:T(8,128)}, u32[]{:S(2)}, u32[]{:S(2)}) collective-permute-start(f32[1024,128]{1,0:T(8,128)} %copy-done.3), channel_id=1, source_target_pairs={{0,1},{1,0},{4,5},{5,4},{8,9},{9,8},{12,13},{13,12},{16,17},{17,16... | collective-permute-start | bytes 1572872 | tf_op jit(solution)/shard_map/ppermute | solution.py:74
  235.8 3.1 collective-permute-done.21
  239.2 5.3 convolution_bitcast_fusion.4
  244.5 9.4 %collective-permute-start.23 = (f32[512,128]{1,0:T(8,128)S(1)}, f32[512,128]{1,0:T(8,128)S(1)}, u32[]{:S(2)}, u32[]{:S(2)}) collective-permute-start(f32[512,128]{1,0:T(8,128)S(1)} %convolution_bitcast_fusion.4), channel_id=1, source_target_pairs={{0,1},{1,0},{2,3},{3,2},{4,5},{5,4},{6,7},{7,6},{8,9},{9,8},{10,11... | collective-permute-start | bytes 786440 | tf_op jit(solution)/shard_map/ppermute | solution.py:74
  253.9 8.9 %collective-permute-start.24 = (f32[512,128]{1,0:T(8,128)S(1)}, f32[512,128]{1,0:T(8,128)S(1)}, u32[]{:S(2)}, u32[]{:S(2)}) collective-permute-start(f32[512,128]{1,0:T(8,128)S(1)} %convolution_bitcast_fusion.4), channel_id=1, source_target_pairs={{0,2},{1,3},{2,0},{3,1},{4,6},{5,7},{6,4},{7,5},{8,10},{9,11},{10,... | collective-permute-start | bytes 786440 | tf_op jit(solution)/shard_map/ppermute | solution.py:74
  262.8 8.9 %collective-permute-start.25 = (f32[512,128]{1,0:T(8,128)S(1)}, f32[512,128]{1,0:T(8,128)S(1)}, u32[]{:S(2)}, u32[]{:S(2)}) collective-permute-start(f32[512,128]{1,0:T(8,128)S(1)} %convolution_bitcast_fusion.4), channel_id=1, source_target_pairs={{0,3},{1,2},{2,1},{3,0},{4,7},{5,6},{6,5},{7,4},{8,11},{9,10},{10,... | collective-permute-start | bytes 786440 | tf_op jit(solution)/shard_map/ppermute | solution.py:74
  271.7 12.9 %collective-permute-done.25 = f32[512,128]{1,0:T(8,128)S(1)} collective-permute-done((f32[512,128]{1,0:T(8,128)S(1)}, f32[512,128]{1,0:T(8,128)S(1)}, u32[]{:S(2)}, u32[]{:S(2)}) %collective-permute-start.25) | collective-permute-done | bytes 262176 | tf_op jit(solution)/shard_map/ppermute | solution.py:74
  284.8 6.3 fusion.10
  292.1 10.9 %collective-permute-start.30 = (f32[512,256]{1,0:T(8,128)S(1)}, f32[512,256]{1,0:T(8,128)S(1)}, u32[]{:S(2)}, u32[]{:S(2)}) collective-permute-start(f32[512,256]{1,0:T(8,128)S(1)} %get-tuple-element.33), channel_id=1, source_target_pairs={{4,100},{5,101},{6,102},{7,103},{12,108},{13,109},{14,110},{15,111... | collective-permute-start | bytes 1572872 | tf_op jit(solution)/shard_map/ppermute | solution.py:74
  303.0 9.5 %collective-permute-start.31 = (f32[512,256]{1,0:T(8,128)S(1)}, f32[512,256]{1,0:T(8,128)S(1)}, u32[]{:S(2)}, u32[]{:S(2)}) collective-permute-start(f32[512,256]{1,0:T(8,128)S(1)} %get-tuple-element.36), channel_id=1, source_target_pairs={{4,2},{5,3},{6,0},{7,1},{12,10},{13,11},{14,8},{15,9},{20,18},{21,... | collective-permute-start | bytes 1572872 | tf_op jit(solution)/shard_map/ppermute | solution.py:74
  312.6 9.6 %collective-permute-start.32 = (f32[512,256]{1,0:T(8,128)S(1)}, f32[512,256]{1,0:T(8,128)S(1)}, u32[]{:S(2)}, u32[]{:S(2)}) collective-permute-start(f32[512,256]{1,0:T(8,128)S(1)} %get-tuple-element.35), channel_id=1, source_target_pairs={{4,98},{5,99},{6,96},{7,97},{12,106},{13,107},{14,104},{15,105},{2... | collective-permute-start | bytes 1572872 | tf_op jit(solution)/shard_map/ppermute | solution.py:74
  322.2 5.6 collective-permute-done.31
  327.7 11.2 %collective-permute-done.32 = f32[512,256]{1,0:T(8,128)S(1)} collective-permute-done((f32[512,256]{1,0:T(8,128)S(1)}, f32[512,256]{1,0:T(8,128)S(1)}, u32[]{:S(2)}, u32[]{:S(2)}) %collective-permute-start.32) | collective-permute-done | bytes 524320 | tf_op jit(solution)/shard_map/ppermute | solution.py:74
  340.2 1.7 fusion.27
  343.2 4.0 select_maximum_fusion
  347.7 2.4 pad_maximum_fusion
  350.1 62.6 %all-gather.23.cloned.1.call-done = f32[8192,256]{1,0:T(8,128)} async-done(((f32[512,256]{1,0:T(8,128)}), f32[8192,256]{1,0:T(8,128)}) %all-gather.23.cloned.1.call-update) | async-done | bytes 8388624 | tf_op jit(solution)/shard_map/all_gather | solution.py:95
  412.7 10.6 %convolution_bitcast_fusion.2 = f32[512,256]{1,0:T(8,128)} fusion(f32[16,512,256]{2,1,0:T(8,128)} %bitcast.66, f32[16,256,256]{2,1,0:T(8,128)} %bitcast.68), kind=kOutput, calls=%fused_computation.19 | convolution fusion | flops 6442450944 | bytes 13107200 | tf_op jit(solution)/shard_map/dot_general | solution.py:21
  423.4 8.5 %collective-permute-start.27 = (f32[512,128]{1,0:T(8,128)S(1)}, f32[512,128]{1,0:T(8,128)S(1)}, u32[]{:S(2)}, u32[]{:S(2)}) collective-permute-start(f32[512,128]{1,0:T(8,128)S(1)} %copy-done.12), channel_id=1, source_target_pairs={{4,2},{5,3},{6,0},{7,1},{12,10},{13,11},{14,8},{15,9},{20,18},{21,... | collective-permute-start | bytes 786440 | tf_op jit(solution)/shard_map/ppermute | solution.py:74
  431.9 9.6 %collective-permute-start.28 = (f32[512,128]{1,0:T(8,128)S(1)}, f32[512,128]{1,0:T(8,128)S(1)}, u32[]{:S(2)}, u32[]{:S(2)}) collective-permute-start(f32[512,128]{1,0:T(8,128)S(1)} %copy-done.10), channel_id=1, source_target_pairs={{4,0},{5,1},{12,8},{13,9},{20,16},{21,17},{28,24},{29,25},{36,32},... | collective-permute-start | bytes 786440 | tf_op jit(solution)/shard_map/ppermute | solution.py:74
  441.4 1.3 collective-permute-done.27
  444.4 1.4 collective-permute-start.26
  445.8 4.5 collective-permute-start.35
  451.0 19.1 %collective-permute-start.41 = (f32[512,128]{1,0:T(8,128)S(1)}, f32[512,128]{1,0:T(8,128)S(1)}, u32[]{:S(2)}, u32[]{:S(2)}) collective-permute-start(f32[512,128]{1,0:T(8,128)S(1)} %copy-done.10), channel_id=1, source_target_pairs={{98,2},{99,3},{102,70},{103,71},{106,10},{107,11},{110,78},{111,79... | collective-permute-start | bytes 786440 | tf_op jit(solution)/shard_map/ppermute | solution.py:74
  470.1 2.4 fusion.26
  472.8 1.5 copy.8
  474.5 42.8 %all-gather.31.cloned.1.call-done = f32[8192,128]{1,0:T(8,128)} async-done(((f32[512,128]{1,0:T(8,128)}), f32[8192,128]{1,0:T(8,128)}) %all-gather.31.cloned.1.call-update) | async-done | bytes 4194320 | tf_op jit(solution)/shard_map/all_gather | solution.py:165
  517.3 5.5 convolution_bitcast_fusion
  522.9 47.4 %all-gather.21.cloned.1.call-done = f32[8192,128]{1,0:T(8,128)} async-done(((f32[512,128]{1,0:T(8,128)}), f32[8192,128]{1,0:T(8,128)}) %all-gather.21.cloned.1.call-update) | async-done | bytes 4194320 | tf_op jit(solution)/shard_map/all_gather | solution.py:166
  570.3 5.4 fusion.9
  578.5 4.6 collective-permute-start.36
  584.4 7.2 %collective-permute-done.34 = f32[512,128]{1,0:T(8,128)S(1)} collective-permute-done((f32[512,128]{1,0:T(8,128)S(1)}, f32[512,128]{1,0:T(8,128)S(1)}, u32[]{:S(2)}, u32[]{:S(2)}) %collective-permute-start.34) | collective-permute-done | bytes 262176 | tf_op jit(solution)/shard_map/ppermute | solution.py:74
  594.6 11.0 %collective-permute-start.42 = (f32[512,128]{1,0:T(8,128)S(1)}, f32[512,128]{1,0:T(8,128)S(1)}, u32[]{:S(2)}, u32[]{:S(2)}) collective-permute-start(f32[512,128]{1,0:T(8,128)S(1)} %get-tuple-element.49), channel_id=1, source_target_pairs={{100,4},{101,5},{102,6},{103,7},{108,12},{109,13},{110,14},{111,15... | collective-permute-start | bytes 786440 | tf_op jit(solution)/shard_map/ppermute | solution.py:74
  605.7 10.2 %collective-permute-start.43 = (f32[512,128]{1,0:T(8,128)S(1)}, f32[512,128]{1,0:T(8,128)S(1)}, u32[]{:S(2)}, u32[]{:S(2)}) collective-permute-start(f32[512,128]{1,0:T(8,128)S(1)} %get-tuple-element.50), channel_id=1, source_target_pairs={{100,36},{101,37},{102,38},{103,39},{108,44},{109,45},{110,46},{11... | collective-permute-start | bytes 786440 | tf_op jit(solution)/shard_map/ppermute | solution.py:74
  620.3 5.6 collective-permute-done.43
  628.1 5.9 collective-permute-done.46
  638.1 8.6 %collective-permute-done.52 = f32[512,128]{1,0:T(8,128)S(1)} collective-permute-done((f32[512,128]{1,0:T(8,128)S(1)}, f32[512,128]{1,0:T(8,128)S(1)}, u32[]{:S(2)}, u32[]{:S(2)}) %collective-permute-start.52) | collective-permute-done | bytes 262176 | tf_op jit(solution)/shard_map/ppermute | solution.py:74
  646.8 6.3 collective-permute-done.55
  653.2 1.7 maximum_add_fusion
  (148 shorter events, 38.7 us)
Async XLA Ops:
  6.5 232.7 %all-gather.19.cloned.1.call-start = ((), (), s32[]{:S(2)}) async-start(), calls=%async_computation.1 | async-start | bytes 4456448 | tf_op jit(solution)/shard_map/all_gather | solution.py:89
  8.2 4.2 collective-permute-start.12
  9.1 10.1 %collective-permute-start.13 = (f32[512,128]{1,0:T(8,128)S(1)}, f32[512,128]{1,0:T(8,128)S(1)}, u32[]{:S(2)}, u32[]{:S(2)}) collective-permute-start(f32[512,128]{1,0:T(8,128)S(1)} %get-tuple-element.25), channel_id=1, source_target_pairs={{2,34},{3,35},{10,42},{11,43},{18,50},{19,51},{26,58},{27,59},{70,... | collective-permute-start | bytes 786440 | tf_op jit(solution)/shard_map/ppermute | solution.py:74
  10.4 9.5 %collective-permute-start.14 = (f32[512,128]{1,0:T(8,128)S(1)}, f32[512,128]{1,0:T(8,128)S(1)}, u32[]{:S(2)}, u32[]{:S(2)}) collective-permute-start(f32[512,128]{1,0:T(8,128)S(1)} %get-tuple-element.31), channel_id=1, source_target_pairs={{2,66},{3,67},{10,74},{11,75},{18,82},{19,83},{26,90},{27,91},{70,... | collective-permute-start | bytes 786440 | tf_op jit(solution)/shard_map/ppermute | solution.py:74
  11.0 9.5 %collective-permute-start.15 = (f32[512,128]{1,0:T(8,128)S(1)}, f32[512,128]{1,0:T(8,128)S(1)}, u32[]{:S(2)}, u32[]{:S(2)}) collective-permute-start(f32[512,128]{1,0:T(8,128)S(1)} %get-tuple-element.30), channel_id=1, source_target_pairs={{2,98},{3,99},{10,106},{11,107},{18,114},{19,115},{26,122},{27,123... | collective-permute-start | bytes 786440 | tf_op jit(solution)/shard_map/ppermute | solution.py:74
  11.7 8.8 %collective-permute-start.16 = (f32[512,128]{1,0:T(8,128)S(1)}, f32[512,128]{1,0:T(8,128)S(1)}, u32[]{:S(2)}, u32[]{:S(2)}) collective-permute-start(f32[512,128]{1,0:T(8,128)S(1)} %get-tuple-element.29), channel_id=1, source_target_pairs={{2,0},{3,1},{10,8},{11,9},{18,16},{19,17},{26,24},{27,25},{70,4},{... | collective-permute-start | bytes 786440 | tf_op jit(solution)/shard_map/ppermute | solution.py:74
  12.4 8.2 %collective-permute-start.17 = (f32[512,128]{1,0:T(8,128)S(1)}, f32[512,128]{1,0:T(8,128)S(1)}, u32[]{:S(2)}, u32[]{:S(2)}) collective-permute-start(f32[512,128]{1,0:T(8,128)S(1)} %get-tuple-element.28), channel_id=1, source_target_pairs={{2,32},{3,33},{10,40},{11,41},{18,48},{19,49},{26,56},{27,57},{70,... | collective-permute-start | bytes 786440 | tf_op jit(solution)/shard_map/ppermute | solution.py:74
  19.2 1.4 collective-permute-start.18
  19.9 0.7 collective-permute-start.19
  21.4 263.4 %all-gather.17.cloned.1.call-start = ((), (), s32[]{:S(2)}) async-start(), calls=%async_computation | async-start | bytes 4456448 | tf_op jit(solution)/shard_map/all_gather | solution.py:132
  29.3 7.6 %collective-permute-start.3 = (f32[512,512]{1,0:T(8,128)}, f32[512,512]{1,0:T(8,128)S(1)}, u32[]{:S(2)}, u32[]{:S(2)}) collective-permute-start(f32[512,512]{1,0:T(8,128)} %shard_map.17), channel_id=1, source_target_pairs={{8,0},{25,17},{42,34},{59,51},{76,68},{93,85},{110,102},{127,119}} | collective-permute-start | bytes 3145736 | tf_op jit(solution)/shard_map/ppermute | solution.py:74
  30.1 17.8 %collective-permute-start.2 = (f32[1024,512]{1,0:T(8,128)S(1)}, f32[1024,512]{1,0:T(8,128)}, u32[]{:S(2)}, u32[]{:S(2)}) collective-permute-start(f32[1024,512]{1,0:T(8,128)S(1)} %copy-done), channel_id=1, source_target_pairs={{1,9},{9,1},{35,43},{43,35},{69,77},{77,69},{103,111},{111,103}} | collective-permute-start | bytes 6291464 | tf_op jit(solution)/shard_map/ppermute | solution.py:74
  41.9 7.3 %collective-permute-start.4 = (f32[1024,512]{1,0:T(8,128)}, f32[1024,512]{1,0:T(8,128)}, u32[]{:S(2)}, u32[]{:S(2)}) collective-permute-start(f32[1024,512]{1,0:T(8,128)} %pad_maximum_fusion.1), channel_id=1, source_target_pairs={{0,1},{8,9},{34,35},{42,43},{68,69},{76,77},{102,103},{110,111}} | collective-permute-start | bytes 6291464 | tf_op jit(solution)/shard_map/ppermute | solution.py:74
  43.9 15.3 %collective-permute-start = (f32[512,512]{1,0:T(8,128)S(1)}, f32[512,512]{1,0:T(8,128)}, u32[]{:S(2)}, u32[]{:S(2)}) collective-permute-start(f32[512,512]{1,0:T(8,128)S(1)} %copy-done.5), channel_id=1, source_target_pairs={{17,1},{25,9},{51,35},{59,43},{85,69},{93,77},{119,103},{127,111}} | collective-permute-start | bytes 3145736 | tf_op jit(solution)/shard_map/ppermute | solution.py:74
  45.6 13.7 %collective-permute-start.1 = (f32[512,512]{1,0:T(8,128)S(1)}, f32[512,512]{1,0:T(8,128)}, u32[]{:S(2)}, u32[]{:S(2)}) collective-permute-start(f32[512,512]{1,0:T(8,128)S(1)} %copy-done.5), channel_id=1, source_target_pairs={{17,9},{25,1},{51,43},{59,35},{85,77},{93,69},{119,111},{127,103}} | collective-permute-start | bytes 3145736 | tf_op jit(solution)/shard_map/ppermute | solution.py:74
  47.2 18.3 %collective-permute-start.5 = (f32[512,512]{1,0:T(8,128)}, f32[512,512]{1,0:T(8,128)S(1)}, u32[]{:S(2)}, u32[]{:S(2)}) collective-permute-start(f32[512,512]{1,0:T(8,128)} %get-tuple-element.51), channel_id=1, source_target_pairs={{17,9},{51,43},{85,77},{119,111}} | collective-permute-start | bytes 3145736 | tf_op jit(solution)/shard_map/ppermute | solution.py:74
  47.9 17.6 %collective-permute-start.6 = (f32[512,512]{1,0:T(8,128)}, f32[512,512]{1,0:T(8,128)S(1)}, u32[]{:S(2)}, u32[]{:S(2)}) collective-permute-start(f32[512,512]{1,0:T(8,128)} %get-tuple-element.51), channel_id=1, source_target_pairs={{17,1},{51,35},{85,69},{119,103}} | collective-permute-start | bytes 3145736 | tf_op jit(solution)/shard_map/ppermute | solution.py:74
  69.4 101.0 %collective-permute-start.10 = (f32[1024,128]{1,0:T(8,128)S(1)}, f32[1024,128]{1,0:T(8,128)S(1)}, u32[]{:S(2)}, u32[]{:S(2)}) collective-permute-start(f32[1024,128]{1,0:T(8,128)S(1)} %get-tuple-element.38), channel_id=1, source_target_pairs={{0,96},{1,97},{8,104},{9,105},{16,112},{17,113},{24,120},{25,121},... | collective-permute-start | bytes 1572872 | tf_op jit(solution)/shard_map/ppermute | solution.py:74
  139.8 30.7 %collective-permute-start.7 = (f32[1024,128]{1,0:T(8,128)S(1)}, f32[1024,128]{1,0:T(8,128)S(1)}, u32[]{:S(2)}, u32[]{:S(2)}) collective-permute-start(f32[1024,128]{1,0:T(8,128)S(1)} %get-tuple-element.40), channel_id=1, source_target_pairs={{0,0},{1,1},{8,8},{9,9},{16,16},{17,17},{24,24},{25,25},{34,2},{35... | collective-permute-start | bytes 1572872 | tf_op jit(solution)/shard_map/ppermute | solution.py:74
  150.0 26.2 %collective-permute-start.8 = (f32[1024,128]{1,0:T(8,128)S(1)}, f32[1024,128]{1,0:T(8,128)S(1)}, u32[]{:S(2)}, u32[]{:S(2)}) collective-permute-start(f32[1024,128]{1,0:T(8,128)S(1)} %get-tuple-element.37), channel_id=1, source_target_pairs={{0,32},{1,33},{8,40},{9,41},{16,48},{17,49},{24,56},{25,57},{34,34... | collective-permute-start | bytes 1572872 | tf_op jit(solution)/shard_map/ppermute | solution.py:74
  160.2 16.0 %collective-permute-start.9 = (f32[1024,128]{1,0:T(8,128)S(1)}, f32[1024,128]{1,0:T(8,128)S(1)}, u32[]{:S(2)}, u32[]{:S(2)}) collective-permute-start(f32[1024,128]{1,0:T(8,128)S(1)} %get-tuple-element.39), channel_id=1, source_target_pairs={{0,64},{1,65},{8,72},{9,73},{16,80},{17,81},{24,88},{25,89},{34,66... | collective-permute-start | bytes 1572872 | tf_op jit(solution)/shard_map/ppermute | solution.py:74
  176.3 25.5 %collective-permute-start.11 = (f32[512,128]{1,0:T(8,128)S(1)}, f32[512,128]{1,0:T(8,128)S(1)}, u32[]{:S(2)}, u32[]{:S(2)}) collective-permute-start(f32[512,128]{1,0:T(8,128)S(1)} %slice.216), channel_id=1, source_target_pairs={{2,0},{3,1},{6,4},{7,5},{10,8},{11,9},{14,12},{15,13},{18,16},{19,... | collective-permute-start | bytes 786440 | tf_op jit(solution)/shard_map/ppermute | solution.py:74
  202.6 137.7 %all-gather.25.cloned.1.call-start = ((), (), s32[]{:S(2)}) async-start(), calls=%async_computation.4 | async-start | bytes 4718592 | tf_op jit(solution)/shard_map/all_gather | solution.py:152
  203.3 138.6 %all-gather.27.cloned.1.call-start = ((), (), s32[]{:S(2)}) async-start(), calls=%async_computation.5 | async-start | bytes 2359296 | tf_op jit(solution)/shard_map/all_gather | solution.py:153
  203.4 32.4 %collective-permute-start.20 = (f32[1024,128]{1,0:T(8,128)}, f32[1024,128]{1,0:T(8,128)S(1)}, u32[]{:S(2)}, u32[]{:S(2)}) collective-permute-start(f32[1024,128]{1,0:T(8,128)} %copy-done.3), channel_id=1, source_target_pairs={{0,2},{1,3},{4,6},{5,7},{8,10},{9,11},{12,14},{13,15},{16,18},{17,... | collective-permute-start | bytes 1572872 | tf_op jit(solution)/shard_map/ppermute | solution.py:74
  214.6 24.3 %collective-permute-start.21 = (f32[1024,128]{1,0:T(8,128)}, f32[1024,128]{1,0:T(8,128)S(1)}, u32[]{:S(2)}, u32[]{:S(2)}) collective-permute-start(f32[1024,128]{1,0:T(8,128)} %copy-done.3), channel_id=1, source_target_pairs={{0,3},{1,2},{4,7},{5,6},{8,11},{9,10},{12,15},{13,14},{16,19},{17,... | collective-permute-start | bytes 1572872 | tf_op jit(solution)/shard_map/ppermute | solution.py:74
  224.8 14.1 %collective-permute-start.22 = (f32[1024,128]{1,0:T(8,128)}, f32[1024,128]{1,0:T(8,128)}, u32[]{:S(2)}, u32[]{:S(2)}) collective-permute-start(f32[1024,128]{1,0:T(8,128)} %copy-done.3), channel_id=1, source_target_pairs={{0,1},{1,0},{4,5},{5,4},{8,9},{9,8},{12,13},{13,12},{16,17},{17,16... | collective-permute-start | bytes 1572872 | tf_op jit(solution)/shard_map/ppermute | solution.py:74
  244.5 27.2 %collective-permute-start.23 = (f32[512,128]{1,0:T(8,128)S(1)}, f32[512,128]{1,0:T(8,128)S(1)}, u32[]{:S(2)}, u32[]{:S(2)}) collective-permute-start(f32[512,128]{1,0:T(8,128)S(1)} %convolution_bitcast_fusion.4), channel_id=1, source_target_pairs={{0,1},{1,0},{2,3},{3,2},{4,5},{5,4},{6,7},{7,6},{8,9},{9,8},{10,11... | collective-permute-start | bytes 786440 | tf_op jit(solution)/shard_map/ppermute | solution.py:74
  253.9 17.8 %collective-permute-start.24 = (f32[512,128]{1,0:T(8,128)S(1)}, f32[512,128]{1,0:T(8,128)S(1)}, u32[]{:S(2)}, u32[]{:S(2)}) collective-permute-start(f32[512,128]{1,0:T(8,128)S(1)} %convolution_bitcast_fusion.4), channel_id=1, source_target_pairs={{0,2},{1,3},{2,0},{3,1},{4,6},{5,7},{6,4},{7,5},{8,10},{9,11},{10,... | collective-permute-start | bytes 786440 | tf_op jit(solution)/shard_map/ppermute | solution.py:74
  262.8 21.8 %collective-permute-start.25 = (f32[512,128]{1,0:T(8,128)S(1)}, f32[512,128]{1,0:T(8,128)S(1)}, u32[]{:S(2)}, u32[]{:S(2)}) collective-permute-start(f32[512,128]{1,0:T(8,128)S(1)} %convolution_bitcast_fusion.4), channel_id=1, source_target_pairs={{0,3},{1,2},{2,1},{3,0},{4,7},{5,6},{6,5},{7,4},{8,11},{9,10},{10,... | collective-permute-start | bytes 786440 | tf_op jit(solution)/shard_map/ppermute | solution.py:74
  291.2 121.5 %all-gather.23.cloned.1.call-start = ((), (), s32[]{:S(2)}) async-start(), calls=%async_computation.3 | async-start | bytes 8912896 | tf_op jit(solution)/shard_map/all_gather | solution.py:95
  291.4 30.8 %collective-permute-start.29 = (f32[512,256]{1,0:T(8,128)S(1)}, f32[512,256]{1,0:T(8,128)S(1)}, u32[]{:S(2)}, u32[]{:S(2)}) collective-permute-start(f32[512,256]{1,0:T(8,128)S(1)} %get-tuple-element.34), channel_id=1, source_target_pairs={{4,4},{5,5},{6,6},{7,7},{12,12},{13,13},{14,14},{15,15},{20,20},{2... | collective-permute-start | bytes 1572872 | tf_op jit(solution)/shard_map/ppermute | solution.py:74
  292.1 30.1 %collective-permute-start.30 = (f32[512,256]{1,0:T(8,128)S(1)}, f32[512,256]{1,0:T(8,128)S(1)}, u32[]{:S(2)}, u32[]{:S(2)}) collective-permute-start(f32[512,256]{1,0:T(8,128)S(1)} %get-tuple-element.33), channel_id=1, source_target_pairs={{4,100},{5,101},{6,102},{7,103},{12,108},{13,109},{14,110},{15,111... | collective-permute-start | bytes 1572872 | tf_op jit(solution)/shard_map/ppermute | solution.py:74
  303.0 24.7 %collective-permute-start.31 = (f32[512,256]{1,0:T(8,128)S(1)}, f32[512,256]{1,0:T(8,128)S(1)}, u32[]{:S(2)}, u32[]{:S(2)}) collective-permute-start(f32[512,256]{1,0:T(8,128)S(1)} %get-tuple-element.36), channel_id=1, source_target_pairs={{4,2},{5,3},{6,0},{7,1},{12,10},{13,11},{14,8},{15,9},{20,18},{21,... | collective-permute-start | bytes 1572872 | tf_op jit(solution)/shard_map/ppermute | solution.py:74
  312.6 26.4 %collective-permute-start.32 = (f32[512,256]{1,0:T(8,128)S(1)}, f32[512,256]{1,0:T(8,128)S(1)}, u32[]{:S(2)}, u32[]{:S(2)}) collective-permute-start(f32[512,256]{1,0:T(8,128)S(1)} %get-tuple-element.35), channel_id=1, source_target_pairs={{4,98},{5,99},{6,96},{7,97},{12,106},{13,107},{14,104},{15,105},{2... | collective-permute-start | bytes 1572872 | tf_op jit(solution)/shard_map/ppermute | solution.py:74
  339.9 130.1 %all-gather.29.cloned.1.call-start = ((), (), s32[]{:S(2)}) async-start(), calls=%async_computation.6 | async-start | bytes 4718592 | tf_op jit(solution)/shard_map/all_gather | solution.py:167
  423.3 94.0 %all-gather.31.cloned.1.call-start = ((), (), s32[]{:S(2)}) async-start(), calls=%async_computation.7 | async-start | bytes 4456448 | tf_op jit(solution)/shard_map/all_gather | solution.py:165
  423.4 19.4 %collective-permute-start.27 = (f32[512,128]{1,0:T(8,128)S(1)}, f32[512,128]{1,0:T(8,128)S(1)}, u32[]{:S(2)}, u32[]{:S(2)}) collective-permute-start(f32[512,128]{1,0:T(8,128)S(1)} %copy-done.12), channel_id=1, source_target_pairs={{4,2},{5,3},{6,0},{7,1},{12,10},{13,11},{14,8},{15,9},{20,18},{21,... | collective-permute-start | bytes 786440 | tf_op jit(solution)/shard_map/ppermute | solution.py:74
  431.9 10.9 %collective-permute-start.28 = (f32[512,128]{1,0:T(8,128)S(1)}, f32[512,128]{1,0:T(8,128)S(1)}, u32[]{:S(2)}, u32[]{:S(2)}) collective-permute-start(f32[512,128]{1,0:T(8,128)S(1)} %copy-done.10), channel_id=1, source_target_pairs={{4,0},{5,1},{12,8},{13,9},{20,16},{21,17},{28,24},{29,25},{36,32},... | collective-permute-start | bytes 786440 | tf_op jit(solution)/shard_map/ppermute | solution.py:74
  443.7 126.6 %all-gather.21.cloned.1.call-start = ((), (), s32[]{:S(2)}) async-start(), calls=%async_computation.2 | async-start | bytes 4456448 | tf_op jit(solution)/shard_map/all_gather | solution.py:166
  444.4 132.0 %collective-permute-start.26 = (f32[512,128]{1,0:T(8,128)S(1)}, f32[512,128]{1,0:T(8,128)}, u32[]{:S(2)}, u32[]{:S(2)}) collective-permute-start(f32[512,128]{1,0:T(8,128)S(1)} %copy-done.10), channel_id=1, source_target_pairs={{2,2},{3,3},{6,70},{7,71},{10,10},{11,11},{14,78},{15,79},{18,18},... | collective-permute-start | bytes 786440 | tf_op jit(solution)/shard_map/ppermute | solution.py:74
  445.8 132.0 %collective-permute-start.35 = (f32[512,128]{1,0:T(8,128)S(1)}, f32[512,128]{1,0:T(8,128)}, u32[]{:S(2)}, u32[]{:S(2)}) collective-permute-start(f32[512,128]{1,0:T(8,128)S(1)} %copy-done.10), channel_id=1, source_target_pairs={{34,2},{35,3},{38,70},{39,71},{42,10},{43,11},{46,78},{47,79},{50,... | collective-permute-start | bytes 786440 | tf_op jit(solution)/shard_map/ppermute | solution.py:74
  450.3 128.1 %collective-permute-start.38 = (f32[512,128]{1,0:T(8,128)S(1)}, f32[512,128]{1,0:T(8,128)S(1)}, u32[]{:S(2)}, u32[]{:S(2)}) collective-permute-start(f32[512,128]{1,0:T(8,128)S(1)} %copy-done.10), channel_id=1, source_target_pairs={{66,2},{67,3},{70,70},{71,71},{74,10},{75,11},{78,78},{79,79},{82,... | collective-permute-start | bytes 786440 | tf_op jit(solution)/shard_map/ppermute | solution.py:74
  451.0 132.1 %collective-permute-start.41 = (f32[512,128]{1,0:T(8,128)S(1)}, f32[512,128]{1,0:T(8,128)S(1)}, u32[]{:S(2)}, u32[]{:S(2)}) collective-permute-start(f32[512,128]{1,0:T(8,128)S(1)} %copy-done.10), channel_id=1, source_target_pairs={{98,2},{99,3},{102,70},{103,71},{106,10},{107,11},{110,78},{111,79... | collective-permute-start | bytes 786440 | tf_op jit(solution)/shard_map/ppermute | solution.py:74
  575.8 8.0 %collective-permute-start.33 = (f32[512,128]{1,0:T(8,128)S(1)}, f32[512,128]{1,0:T(8,128)S(1)}, u32[]{:S(2)}, u32[]{:S(2)}) collective-permute-start(f32[512,128]{1,0:T(8,128)S(1)} %get-tuple-element.49), channel_id=1, source_target_pairs={{4,4},{5,5},{6,6},{7,7},{12,12},{13,13},{14,14},{15,15},{20,20},{2... | collective-permute-start | bytes 786440 | tf_op jit(solution)/shard_map/ppermute | solution.py:74
  576.5 15.2 %collective-permute-start.34 = (f32[512,128]{1,0:T(8,128)S(1)}, f32[512,128]{1,0:T(8,128)S(1)}, u32[]{:S(2)}, u32[]{:S(2)}) collective-permute-start(f32[512,128]{1,0:T(8,128)S(1)} %get-tuple-element.50), channel_id=1, source_target_pairs={{4,36},{5,37},{6,38},{7,39},{12,44},{13,45},{14,46},{15,47},{20,52... | collective-permute-start | bytes 786440 | tf_op jit(solution)/shard_map/ppermute | solution.py:74
  577.8 16.2 %collective-permute-start.44 = (f32[512,128]{1,0:T(8,128)S(1)}, f32[512,128]{1,0:T(8,128)S(1)}, u32[]{:S(2)}, u32[]{:S(2)}) collective-permute-start(f32[512,128]{1,0:T(8,128)S(1)} %copy-done.10), channel_id=1, source_target_pairs={{0,2},{1,3},{4,70},{5,71},{8,10},{9,11},{12,78},{13,79},{16,18},{1... | collective-permute-start | bytes 786440 | tf_op jit(solution)/shard_map/ppermute | solution.py:74
  578.5 16.2 %collective-permute-start.36 = (f32[512,128]{1,0:T(8,128)S(1)}, f32[512,128]{1,0:T(8,128)S(1)}, u32[]{:S(2)}, u32[]{:S(2)}) collective-permute-start(f32[512,128]{1,0:T(8,128)S(1)} %get-tuple-element.49), channel_id=1, source_target_pairs={{36,4},{37,5},{38,6},{39,7},{44,12},{45,13},{46,14},{47,15},{52,20... | collective-permute-start | bytes 786440 | tf_op jit(solution)/shard_map/ppermute | solution.py:74
  583.1 22.6 %collective-permute-start.37 = (f32[512,128]{1,0:T(8,128)S(1)}, f32[512,128]{1,0:T(8,128)S(1)}, u32[]{:S(2)}, u32[]{:S(2)}) collective-permute-start(f32[512,128]{1,0:T(8,128)S(1)} %get-tuple-element.50), channel_id=1, source_target_pairs={{36,36},{37,37},{38,38},{39,39},{44,44},{45,45},{46,46},{47,47},{5... | collective-permute-start | bytes 786440 | tf_op jit(solution)/shard_map/ppermute | solution.py:74
  583.7 33.1 %collective-permute-start.39 = (f32[512,128]{1,0:T(8,128)S(1)}, f32[512,128]{1,0:T(8,128)S(1)}, u32[]{:S(2)}, u32[]{:S(2)}) collective-permute-start(f32[512,128]{1,0:T(8,128)S(1)} %get-tuple-element.49), channel_id=1, source_target_pairs={{68,4},{69,5},{70,6},{71,7},{76,12},{77,13},{78,14},{79,15},{84,20... | collective-permute-start | bytes 786440 | tf_op jit(solution)/shard_map/ppermute | solution.py:74
  591.7 25.9 %collective-permute-start.40 = (f32[512,128]{1,0:T(8,128)S(1)}, f32[512,128]{1,0:T(8,128)S(1)}, u32[]{:S(2)}, u32[]{:S(2)}) collective-permute-start(f32[512,128]{1,0:T(8,128)S(1)} %get-tuple-element.50), channel_id=1, source_target_pairs={{68,36},{69,37},{70,38},{71,39},{76,44},{77,45},{78,46},{79,47},{8... | collective-permute-start | bytes 786440 | tf_op jit(solution)/shard_map/ppermute | solution.py:74
  593.9 24.9 %collective-permute-start.47 = (f32[512,128]{1,0:T(8,128)S(1)}, f32[512,128]{1,0:T(8,128)S(1)}, u32[]{:S(2)}, u32[]{:S(2)}) collective-permute-start(f32[512,128]{1,0:T(8,128)S(1)} %copy-done.10), channel_id=1, source_target_pairs={{32,2},{33,3},{36,70},{37,71},{40,10},{41,11},{44,78},{45,79},{48,... | collective-permute-start | bytes 786440 | tf_op jit(solution)/shard_map/ppermute | solution.py:74
  594.6 24.9 %collective-permute-start.42 = (f32[512,128]{1,0:T(8,128)S(1)}, f32[512,128]{1,0:T(8,128)S(1)}, u32[]{:S(2)}, u32[]{:S(2)}) collective-permute-start(f32[512,128]{1,0:T(8,128)S(1)} %get-tuple-element.49), channel_id=1, source_target_pairs={{100,4},{101,5},{102,6},{103,7},{108,12},{109,13},{110,14},{111,15... | collective-permute-start | bytes 786440 | tf_op jit(solution)/shard_map/ppermute | solution.py:74
  605.7 20.2 %collective-permute-start.43 = (f32[512,128]{1,0:T(8,128)S(1)}, f32[512,128]{1,0:T(8,128)S(1)}, u32[]{:S(2)}, u32[]{:S(2)}) collective-permute-start(f32[512,128]{1,0:T(8,128)S(1)} %get-tuple-element.50), channel_id=1, source_target_pairs={{100,36},{101,37},{102,38},{103,39},{108,44},{109,45},{110,46},{11... | collective-permute-start | bytes 786440 | tf_op jit(solution)/shard_map/ppermute | solution.py:74
  616.8 10.4 %collective-permute-start.45 = (f32[512,128]{1,0:T(8,128)S(1)}, f32[512,128]{1,0:T(8,128)S(1)}, u32[]{:S(2)}, u32[]{:S(2)}) collective-permute-start(f32[512,128]{1,0:T(8,128)S(1)} %get-tuple-element.49), channel_id=1, source_target_pairs={{0,6},{1,7},{2,4},{3,5},{8,14},{9,15},{10,12},{11,13},{16,22},{17,... | collective-permute-start | bytes 786440 | tf_op jit(solution)/shard_map/ppermute | solution.py:74
  617.5 16.4 %collective-permute-start.46 = (f32[512,128]{1,0:T(8,128)S(1)}, f32[512,128]{1,0:T(8,128)S(1)}, u32[]{:S(2)}, u32[]{:S(2)}) collective-permute-start(f32[512,128]{1,0:T(8,128)S(1)} %get-tuple-element.50), channel_id=1, source_target_pairs={{0,38},{1,39},{2,36},{3,37},{8,46},{9,47},{10,44},{11,45},{16,54},... | collective-permute-start | bytes 786440 | tf_op jit(solution)/shard_map/ppermute | solution.py:74
  618.9 16.4 %collective-permute-start.50 = (f32[512,128]{1,0:T(8,128)S(1)}, f32[512,128]{1,0:T(8,128)S(1)}, u32[]{:S(2)}, u32[]{:S(2)}) collective-permute-start(f32[512,128]{1,0:T(8,128)S(1)} %copy-done.10), channel_id=1, source_target_pairs={{64,2},{65,3},{68,70},{69,71},{72,10},{73,11},{76,78},{77,79},{80,... | collective-permute-start | bytes 786440 | tf_op jit(solution)/shard_map/ppermute | solution.py:74
  619.6 16.4 %collective-permute-start.48 = (f32[512,128]{1,0:T(8,128)S(1)}, f32[512,128]{1,0:T(8,128)S(1)}, u32[]{:S(2)}, u32[]{:S(2)}) collective-permute-start(f32[512,128]{1,0:T(8,128)S(1)} %get-tuple-element.49), channel_id=1, source_target_pairs={{32,6},{33,7},{34,4},{35,5},{40,14},{41,15},{42,12},{43,13},{48,22... | collective-permute-start | bytes 786440 | tf_op jit(solution)/shard_map/ppermute | solution.py:74
  625.9 10.9 %collective-permute-start.49 = (f32[512,128]{1,0:T(8,128)S(1)}, f32[512,128]{1,0:T(8,128)S(1)}, u32[]{:S(2)}, u32[]{:S(2)}) collective-permute-start(f32[512,128]{1,0:T(8,128)S(1)} %get-tuple-element.50), channel_id=1, source_target_pairs={{32,38},{33,39},{34,36},{35,37},{40,46},{41,47},{42,44},{43,45},{4... | collective-permute-start | bytes 786440 | tf_op jit(solution)/shard_map/ppermute | solution.py:74
  627.3 10.8 %collective-permute-start.51 = (f32[512,128]{1,0:T(8,128)S(1)}, f32[512,128]{1,0:T(8,128)S(1)}, u32[]{:S(2)}, u32[]{:S(2)}) collective-permute-start(f32[512,128]{1,0:T(8,128)S(1)} %get-tuple-element.49), channel_id=1, source_target_pairs={{64,6},{65,7},{66,4},{67,5},{72,14},{73,15},{74,12},{75,13},{80,22... | collective-permute-start | bytes 786440 | tf_op jit(solution)/shard_map/ppermute | solution.py:74
  634.0 12.7 %collective-permute-start.52 = (f32[512,128]{1,0:T(8,128)S(1)}, f32[512,128]{1,0:T(8,128)S(1)}, u32[]{:S(2)}, u32[]{:S(2)}) collective-permute-start(f32[512,128]{1,0:T(8,128)S(1)} %get-tuple-element.50), channel_id=1, source_target_pairs={{64,38},{65,39},{66,36},{67,37},{72,46},{73,47},{74,44},{75,45},{8... | collective-permute-start | bytes 786440 | tf_op jit(solution)/shard_map/ppermute | solution.py:74
  635.3 11.4 %collective-permute-start.53 = (f32[512,128]{1,0:T(8,128)S(1)}, f32[512,128]{1,0:T(8,128)S(1)}, u32[]{:S(2)}, u32[]{:S(2)}) collective-permute-start(f32[512,128]{1,0:T(8,128)S(1)} %copy-done.10), channel_id=1, source_target_pairs={{96,2},{97,3},{100,70},{101,71},{104,10},{105,11},{108,78},{109,79... | collective-permute-start | bytes 786440 | tf_op jit(solution)/shard_map/ppermute | solution.py:74
  636.0 10.7 %collective-permute-start.54 = (f32[512,128]{1,0:T(8,128)S(1)}, f32[512,128]{1,0:T(8,128)S(1)}, u32[]{:S(2)}, u32[]{:S(2)}) collective-permute-start(f32[512,128]{1,0:T(8,128)S(1)} %get-tuple-element.49), channel_id=1, source_target_pairs={{96,6},{97,7},{98,4},{99,5},{104,14},{105,15},{106,12},{107,13},{1... | collective-permute-start | bytes 786440 | tf_op jit(solution)/shard_map/ppermute | solution.py:74
  636.8 16.3 %collective-permute-start.55 = (f32[512,128]{1,0:T(8,128)S(1)}, f32[512,128]{1,0:T(8,128)S(1)}, u32[]{:S(2)}, u32[]{:S(2)}) collective-permute-start(f32[512,128]{1,0:T(8,128)S(1)} %get-tuple-element.50), channel_id=1, source_target_pairs={{96,38},{97,39},{98,36},{99,37},{104,46},{105,47},{106,44},{107,45... | collective-permute-start | bytes 786440 | tf_op jit(solution)/shard_map/ppermute | solution.py:74
  (13 other events, 169.1 us)
Sparse Core Ops, SparseCore 0:
  21.6 80.9 all-gather.18
  202.7 54.1 all-gather.16
  258.6 35.5 all-gather.24
  295.8 26.9 all-gather.26
  340.1 72.5 all-gather.22
  423.5 39.1 all-gather.28
  464.8 52.5 all-gather.30
  519.5 50.7 all-gather.20

commit v2 on v0

v2 whole, which is shorter than its diff:
```python
import functools

import jax
import jax.numpy as jnp
from jax import lax
from jax.experimental import pallas as pl
from jax.experimental.pallas import tpu as pltpu
from jax.sharding import Mesh, PartitionSpec as P

F32 = jnp.float32
AXES = ("z", "y", "x", "core")
RING = 4
SUB = 128
LEAF = 4 * SUB
MESH = pl.DeviceIdType.MESH
VMEM = pl.BlockSpec(memory_space=pltpu.VMEM)


def dot(left, right):
    return jnp.dot(left, right, precision=lax.Precision.HIGHEST, preferred_element_type=F32)


def dot_blocks(left, right):
    return lax.dot_general(left, right, (((0, 2), (0, 1)), ((), ())), precision=lax.Precision.HIGHEST, preferred_element_type=F32)


def here():
    return tuple(lax.axis_index(a) for a in AXES)


def turn(i, d):
    return lax.rem(i + d + RING, RING)


def enter(peers):
    barrier = pltpu.get_barrier_semaphore()
    for peer in peers:
        pl.semaphore_signal(barrier, inc=1, device_id=peer, device_id_type=MESH)
    pl.semaphore_wait(barrier, len(peers))


def call(kernel, shapes, scratch, ident, *args):
    return pl.pallas_call(
        kernel,
        out_shape=[jax.ShapeDtypeStruct(s, F32) for s in shapes],
        in_specs=[VMEM] * len(args),
        out_specs=[VMEM] * len(shapes),
        scratch_shapes=scratch,
        compiler_params=pltpu.CompilerParams(collective_id=ident, has_side_effects=True),
        name=kernel.__name__,
    )(*args)


def sems(n):
    return [pltpu.SemaphoreType.DMA((n,)), pltpu.SemaphoreType.DMA((n,))]


class Link:
    def __init__(self, send, recv, base=0):
        self.send, self.recv, self.base = send, recv, base

    def copy(self, i, src, dst, dev, recv=None):
        j = i if recv is None else recv
        return pltpu.make_async_remote_copy(
            src_ref=src, dst_ref=dst, send_sem=self.send.at[self.base + i], recv_sem=self.recv.at[self.base + j], device_id=dev, device_id_type=MESH
        )


def matmul(out, left, right, sign=1.0, add=None, rows=2 * SUB):
    def step(i, _):
        tile = pl.ds(pl.multiple_of(i * rows, rows), rows)
        prod = dot(left[tile, :], right[...])
        prod = prod if sign > 0 else -prod
        out[tile, :] = prod if add is None else add[tile, :] + prod
        return 0

    lax.fori_loop(0, left.shape[0] // rows, step, 0)


def invert_leaf(m_ref, o_ref):
    rows = lax.broadcasted_iota(jnp.int32, (SUB, SUB), 0)
    cols = lax.broadcasted_iota(jnp.int32, (SUB, SUB), 1)
    eye = (rows == cols).astype(F32)
    o_ref[...] = jnp.zeros(o_ref.shape, F32)
    powers, sums, recips = [], [], []
    for b in range(LEAF // SUB):
        s = slice(b * SUB, (b + 1) * SUB)
        blk = m_ref[s, s]
        diag = jnp.where(rows == cols, blk, 0.0)
        recip_col = 1.0 / jnp.sum(diag, axis=1, keepdims=True)
        recips.append(1.0 / jnp.sum(diag, axis=0, keepdims=True))
        strict = jnp.where(rows > cols, blk, 0.0) * recip_col
        sums.append(eye - strict)
        powers.append(dot(strict, strict))
    steps = SUB.bit_length() - 2
    for i in range(steps):
        sums = [p + dot(p, q) for p, q in zip(sums, powers)]
        if i < steps - 1:
            powers = [dot(q, q) for q in powers]
    for b in range(LEAF // SUB):
        s = slice(b * SUB, (b + 1) * SUB)
        o_ref[s, s] = sums[b] * recips[b]
    size = SUB
    while size < LEAF:
        prods = []
        for lo in range(0, LEAF, 2 * size):
            a, c = slice(lo, lo + size), slice(lo + size, lo + 2 * size)
            prods.append((a, c, dot(m_ref[c, a], o_ref[a, a])))
        for a, c, t in prods:
            o_ref[c, a] = -dot(o_ref[c, c], t)
        size *= 2


def leaves(t_ref, inv, nb, near, l_next, c_next, c3, c4, m_ref, send, recv, local):
    z, y, x, k = here()
    link = Link(send, recv)
    on = z == x
    mine = on & (y // 2 == k)
    pair_y = y + 1 - 2 * lax.rem(y, 2)
    peers = [{"z": turn(z, d), "x": px} for px in (x, 3 - x) for d in range(RING) if not (d == 0 and px is x)]
    peers += [{"y": turn(y, d)} for d in range(1, RING)]
    enter(peers)
    low = slice(LEAF, 2 * LEAF)
    c_src, l_src = on & (k == 1) & (y == 1), on & (k == 1) & (y == 2)
    c_copy = link.copy(0, t_ref, c_next, {"y": turn(y, -1)})
    l_copy = link.copy(1, t_ref.at[low, :], l_next, {"y": turn(y, 1)})
    pl.when(c_src)(lambda: c_copy.start())
    pl.when(l_src)(lambda: l_copy.start())

    src3 = (lax.rem(x, 2) == 1) & (z == x - 1)
    copies3 = []
    for h in range(2):
        for d in range(RING):
            q = turn(z, d)
            piece = t_ref.at[h * LEAF:(h + 1) * LEAF, pl.ds(pl.multiple_of(q * SUB, SUB), SUB)]
            if h == 0 and d == 0:
                own3 = pltpu.make_async_copy(piece, c3, local.at[0])
            else:
                copies3.append(link.copy(4 + len(copies3), piece, c3, {"z": q, "x": 3 - x if h else x}, recv=4))

    @pl.when(src3)
    def _():
        for c in copies3:
            c.start()
        own3.start()

    src4 = (x >= 2) & (z < 2)
    copies4 = []
    for h in range(2):
        for p in range(2):
            piece = t_ref.at[h * LEAF:(h + 1) * LEAF, 2 * SUB * p:2 * SUB * (p + 1)]
            if h == 0 and p == 0:
                own4 = pltpu.make_async_copy(piece, c4, local.at[1])
            else:
                copies4.append(link.copy(11 + len(copies4), piece, c4, {"z": 3 - z if p else z, "x": 3 - x if h else x}, recv=5))

    @pl.when(src4)
    def _():
        for c in copies4:
            c.start()
        own4.start()

    inv_pair = link.copy(2, inv, nb, {"y": pair_y})
    inv_near = link.copy(3, inv, near, {"y": 3 - y})
    near_src, near_dst = on & (k == 1) & (y >= 2), on & (k == 1) & (y < 2)

    @pl.when(mine)
    def _():
        half = pl.ds(pl.multiple_of(lax.rem(y, 2) * LEAF, LEAF), LEAF)
        m_ref[...] = t_ref[half, :]
        invert_leaf(m_ref, inv)
        inv_pair.start()
        pl.when(near_src)(lambda: inv_near.start())
        inv_pair.wait()
        pl.when(near_src)(lambda: inv_near.wait_send())

    pl.when(near_dst)(lambda: inv_near.wait_recv())
    pl.when(c_src)(lambda: c_copy.wait_send())
    pl.when(l_src)(lambda: l_copy.wait_send())
    pl.when(on & (k == 1) & (y == 0))(lambda: c_copy.wait_recv())
    pl.when(on & (k == 1) & (y == 3))(lambda: l_copy.wait_recv())

    @pl.when(src3)
    def _():
        for c in copies3:
            c.wait_send()
        own3.wait()

    @pl.when(src4)
    def _():
        for c in copies4:
            c.wait_send()
        own4.wait()

    pl.when(jnp.logical_not(src3))(lambda: copies3[0].wait_recv())
    pl.when(jnp.logical_not(src4))(lambda: link.copy(11, t_ref.at[:LEAF, :2 * SUB], c4, {"z": z}, recv=5).wait_recv())


def diagonal(t_ref, inv, nb, near, l_next, c_next, dg, x10, a_buf, far, x32, tmp, prod, send, recv):
    z, y, x, k = here()
    link = Link(send, recv)
    enter([{"y": turn(y, d)} for d in range(1, RING)] + [{"core": 1 - k}])
    low, up = slice(LEAF, 2 * LEAF), slice(0, LEAF)

    @pl.when(z == x)
    def _():
        dg[...] = jnp.zeros(dg.shape, F32)
        fwd = link.copy(0, nb, far, {"y": 3 - y})
        a_first = link.copy(1, inv, a_buf.at[0], {"core": 1 - k})
        a_second = link.copy(2, x10, a_buf.at[1], {"core": 1 - k})
        x_far = link.copy(3, x10, x32, {"y": 3 - y})
        b_side, a_side, work = (k == 1) & (y >= 2), (k == 0) & (y < 2), (k == 1) & (y < 2)
        pl.when(b_side)(lambda: fwd.start())
        pl.when(a_side)(lambda: a_first.start())

        @pl.when(y == 2 * k)
        def _():
            matmul(tmp, t_ref.at[low, :], inv)
            matmul(x10, nb, tmp, -1.0)
            pl.when(k == 0)(lambda: a_second.start())
            pl.when(k == 1)(lambda: x_far.start())
            dg[up, :] = inv[...]
            dg[low, :] = x10[...]

        @pl.when((k == 1) & (y == 3))
        def _():
            matmul(tmp, l_next, nb)
            matmul(x10, inv, tmp, -1.0)
            x_far.start()

        @pl.when(y == 2 * k + 1)
        def _():
            dg[low, :] = inv[...]

        @pl.when(work)
        def _():
            a_first.wait_recv()
            matmul(prod, t_ref, a_buf.at[0])

            @pl.when(y == 0)
            def _():
                a_second.wait_recv()
                matmul(prod, c_next, a_buf.at[1], add=prod)
                matmul(dg.at[low, :], near, prod.at[low, :], -1.0)
                fwd.wait_recv()
                matmul(dg.at[up, :], far, prod.at[up, :], -1.0)

            @pl.when(y == 1)
            def _():
                matmul(dg.at[up, :], near, prod.at[up, :], -1.0)
                fwd.wait_recv()
                matmul(dg.at[low, :], far, prod.at[low, :], -1.0)

            x_far.wait_recv()
            matmul(dg.at[low, :], x32, prod.at[up, :], -1.0, add=dg.at[low, :])

        @pl.when(b_side)
        def _():
            fwd.wait_send()
            x_far.wait_send()

        pl.when(a_side)(lambda: a_first.wait_send())
        pl.when((k == 0) & (y == 0))(lambda: a_second.wait_send())


def run(*stages):
    stages = list(stages)
    while stages:
        for s in list(stages):
            try:
                next(s)
            except StopIteration:
                stages.remove(s)


def ring_stages(link, axis, pos, block, spare):
    left, right = {axis: turn(pos, -1)}, {axis: turn(pos, 1)}
    own = block(pos)
    to_right, to_left = link.copy(0, own, own, right), link.copy(1, own, own, left)
    to_right.start()
    to_left.start()
    yield
    from_left, from_right = block(turn(pos, -1)), block(turn(pos, 1))
    link.copy(0, from_left, from_left, right).wait_recv()
    half0 = spare(turn(pos, -1), 0)
    on_right = link.copy(2, half0, half0, right)
    on_right.start()
    link.copy(1, from_right, from_right, left).wait_recv()
    half1 = spare(turn(pos, 1), 1)
    on_left = link.copy(3, half1, half1, left)
    on_left.start()
    yield
    far0, far1 = spare(turn(pos, 2), 0), spare(turn(pos, 2), 1)
    link.copy(2, far0, far0, right).wait_recv()
    link.copy(3, far1, far1, left).wait_recv()
    for c in (to_right, to_left, on_right, on_left):
        c.wait_send()


def plane_gather(ref, z, y, send, recv, base):
    n = ref.shape[2]
    spans = [pl.ds(c * (n // 2), n // 2) for c in range(2)]

    def quarter(c, half):
        return pl.ds(c * (n // 2) + half * (n // 4), n // 4)

    first = [
        ring_stages(Link(send, recv, base), "y", y, lambda i: ref.at[z, i, spans[0], :], lambda i, h: ref.at[z, i, quarter(0, h), :]),
        ring_stages(Link(send, recv, base + 4), "z", z, lambda i: ref.at[i, y, spans[1], :], lambda i, h: ref.at[i, y, quarter(1, h), :]),
    ]
    for _ in range(2):
        for s in first:
            next(s)
        yield
    for s in first:
        next(s, None)
    second = [
        ring_stages(Link(send, recv, base + 8), "z", z, lambda i: ref.at[i, :, spans[0], :], lambda i, h: ref.at[i, :, quarter(0, h), :]),
        ring_stages(Link(send, recv, base + 12), "y", y, lambda i: ref.at[:, i, spans[1], :], lambda i, h: ref.at[:, i, quarter(1, h), :]),
    ]
    for _ in range(2):
        for s in second:
            next(s)
        yield
    for s in second:
        next(s, None)


def team_gather(ref, x, k, send, recv, base):
    link = Link(send, recv, base)
    n = ref.shape[1]
    halves = [pl.ds(h * (n // 2), n // 2) for h in range(2)]
    left, right, flip = {"x": turn(x, -1)}, {"x": turn(x, 1)}, {"core": 1 - k}

    def blk(d, core):
        return ref.at[2 * turn(x, d) + core]

    def part(d, core, h):
        return ref.at[2 * turn(x, d) + core, halves[h], :]

    def same(i, view, dev):
        return link.copy(i, view, view, dev)

    sent = [same(0, blk(0, k), right), same(1, blk(0, k), left), same(2, blk(0, k), flip)]
    for c in sent:
        c.start()
    yield
    same(0, blk(-1, k), right).wait_recv()
    more = [same(3, part(-1, k, 0), right), same(4, blk(-1, k), flip)]
    for c in more:
        c.start()
    sent += more
    same(1, blk(1, k), left).wait_recv()
    more = [same(5, part(1, k, 1), left), same(6, blk(1, k), flip)]
    for c in more:
        c.start()
    sent += more
    yield
    same(3, part(2, k, 0), right).wait_recv()
    more = [same(7, part(2, k, 0), flip)]
    same(5, part(2, k, 1), left).wait_recv()
    more.append(same(8, part(2, k, 1), flip))
    for c in more:
        c.start()
    sent += more
    yield
    same(2, blk(0, 1 - k), flip).wait_recv()
    same(4, blk(-1, 1 - k), flip).wait_recv()
    same(6, blk(1, 1 - k), flip).wait_recv()
    same(7, part(2, 1 - k, 0), flip).wait_recv()
    same(8, part(2, 1 - k, 1), flip).wait_recv()
    for c in sent:
        c.wait_send()


def ring_peers(*axes):
    return [{a: turn(lax.axis_index(a), d)} for a in axes for d in (1, -1)]


def spread(dg, team, hop, rows, send, recv, local):
    z, y, x, k = here()
    link = Link(send, recv)
    enter([{"z": turn(z, d)} for d in range(1, RING)] + ring_peers("y", "x") + [{"core": 1 - k}])
    slot = 2 * x + k

    def column(q):
        return dg.at[:, pl.ds(pl.multiple_of(q * SUB, SUB), SUB)]

    out = [link.copy(d, column(turn(z, d)), team.at[slot], {"z": turn(z, d)}, recv=0) for d in range(1, RING)]
    own = pltpu.make_async_copy(column(z), team.at[slot], local.at[0])

    @pl.when(z == x)
    def _():
        for c in (out[0], out[2], out[1]):
            c.start()
        own.start()
        own.wait()

    pl.when(z != x)(lambda: out[0].wait_recv())
    cross = link.copy(4, team.at[slot, LEAF:, :], hop, {"x": 3 - x})
    cross.start()
    gather = team_gather(team, x, k, send, recv, 5)
    next(gather)
    take = pltpu.make_async_copy(team.at[slot, :LEAF, :], rows.at[z, y], local.at[1])
    odd = lax.rem(x, 2) == 1

    @pl.when(odd)
    def _():
        take.start()
        take.wait()

    cross.wait_recv()
    take_hop = pltpu.make_async_copy(hop, rows.at[z, y], local.at[1])

    @pl.when(jnp.logical_not(odd))
    def _():
        take_hop.start()
        take_hop.wait()

    run(plane_gather(rows, z, y, send, recv, 14), gather)
    cross.wait_send()

    @pl.when(z == x)
    def _():
        for c in out:
            c.wait_send()


def swap(t_ref, full, send, recv, local):
    z, y, x, k = here()
    link = Link(send, recv)
    enter([{"x": 3 - x}, {"core": 1 - k}])
    even = 1 - lax.rem(x, 2)
    mine, theirs = 2 * k + even, 2 * k + 1 - even
    cross = link.copy(0, t_ref, full.at[mine], {"x": 3 - x})
    flip = link.copy(1, t_ref, full.at[mine], {"core": 1 - k})
    own = pltpu.make_async_copy(t_ref, full.at[mine], local.at[0])
    for c in (cross, flip, own):
        c.start()
    cross.wait_recv()
    on = link.copy(2, full.at[theirs], full.at[theirs], {"core": 1 - k})
    on.start()
    own.wait()
    flip.wait_recv()
    on.wait_recv()
    for c in (cross, flip, on):
        c.wait_send()


def team_only(tile, team, send, recv, local):
    z, y, x, k = here()
    enter(ring_peers("x") + [{"core": 1 - k}])
    own = pltpu.make_async_copy(tile, team.at[2 * x + k], local.at[0])
    own.start()
    own.wait()
    run(team_gather(team, x, k, send, recv, 0))


def team_and_plane(tile, block, team, plane, send, recv, local):
    z, y, x, k = here()
    enter(ring_peers("z", "y", "x") + [{"core": 1 - k}])
    own = pltpu.make_async_copy(tile, team.at[2 * x + k], local.at[0])
    own_block = pltpu.make_async_copy(block, plane.at[z, y], local.at[1])
    own.start()
    own_block.start()
    own.wait()
    own_block.wait()
    run(plane_gather(plane, z, y, send, recv, 9), team_gather(team, x, k, send, recv, 0))


def place(dg, x3, x4, out, send, recv, local):
    z, y, x, k = here()
    link = Link(send, recv)
    peers = [{"z": turn(z, d), "x": px} for px in (x, 3 - x) for d in range(RING) if not (d == 0 and px is x)]
    enter(peers)

    def spot(h, q):
        return out.at[pl.ds(pl.multiple_of(h * LEAF, LEAF), LEAF), pl.ds(pl.multiple_of(q * SUB, SUB), SUB)]

    odd = lax.rem(x, 2) == 1
    h3 = jnp.where(odd, 0, 1)
    i3 = jnp.where(odd, x, 3 - x)
    h4 = jnp.where(x >= 2, 0, 1)
    i4 = jnp.where(x >= 2, x, 3 - x)
    jobs = [(x3, h3, i3, i3 - 1)] + [(x4.at[:, j * SUB:(j + 1) * SUB], h4, i4, j) for j in range(2)]
    for n, (src, h, i, zz) in enumerate(jobs):
        stay = (i == x) & (zz == z)
        go = pltpu.make_async_remote_copy(
            src_ref=src, dst_ref=spot(h, z), send_sem=send.at[n], recv_sem=recv.at[h * RING + z], device_id={"z": zz, "x": i}, device_id_type=MESH
        )
        keep = pltpu.make_async_copy(src, spot(h, z), local.at[0])
        pl.when(jnp.logical_not(stay))(lambda go=go: go.start())
        pl.when(stay)(lambda keep=keep: keep.start())

    keep_d = pltpu.make_async_copy(dg, out, local.at[1])

    @pl.when(z == x)
    def _():
        keep_d.start()
        keep_d.wait()

    @pl.when(z > x)
    def _():
        out[...] = jnp.zeros(out.shape, F32)

    target = (odd & (z == x - 1)) | ((x >= 2) & (z < 2))

    @pl.when(target)
    def _():
        for h in range(2):
            for d in range(RING):
                q = turn(z, d)
                if h == 0 and d == 0:
                    pltpu.make_async_copy(x3, spot(0, z), local.at[0]).wait()
                else:
                    pltpu.make_async_remote_copy(
                        src_ref=x3, dst_ref=spot(h, q), send_sem=send.at[0], recv_sem=recv.at[h * RING + q], device_id={"z": z}, device_id_type=MESH
                    ).wait_recv()

    for n, (src, h, i, zz) in enumerate(jobs):
        stay = (i == x) & (zz == z)
        go = pltpu.make_async_remote_copy(
            src_ref=src, dst_ref=spot(h, z), send_sem=send.at[n], recv_sem=recv.at[h * RING + z], device_id={"z": zz, "x": i}, device_id_type=MESH
        )
        pl.when(jnp.logical_not(stay))(lambda go=go: go.wait_send())


def by_zy(mat):
    n = mat.shape[1]
    return mat.reshape(RING, RING, SUB, n).transpose(1, 0, 2, 3).reshape(RING * RING, SUB, n)


def invert(t):
    x, k = lax.axis_index("x"), lax.axis_index("core")
    inner = (x == 1) | (x == 2)
    dma2 = pltpu.SemaphoreType.DMA((2,))
    leaf, tile = (LEAF, LEAF), (2 * LEAF, LEAF)
    inv, nb, near, l_next, c_next, c3, c4 = call(
        leaves, [leaf, leaf, leaf, leaf, tile, (LEAF, SUB), (LEAF, 2 * SUB)], [pltpu.VMEM(leaf, F32)] + sems(14) + [dma2], 0, t
    )
    g3 = lax.all_gather(c3, ("z", "y"), axis=0)
    g4 = lax.all_gather(c4, ("z", "y"), axis=0)
    scratch = [pltpu.VMEM(leaf, F32), pltpu.VMEM((2,) + leaf, F32), pltpu.VMEM(leaf, F32), pltpu.VMEM(leaf, F32), pltpu.VMEM(leaf, F32), pltpu.VMEM(tile, F32)]
    (dg,) = call(diagonal, [tile], scratch + sems(4), 1, t, inv, nb, near, l_next, c_next)
    team_d, hop, rows3 = call(spread, [(8, 2 * LEAF, SUB), (LEAF, SUB), (RING, RING, LEAF, SUB)], sems(30) + [dma2], 2, dg)
    rows3 = rows3.reshape(16, LEAF, SUB)

    ds = lax.dynamic_slice_in_dim(team_d, jnp.where(inner, 0, 4), 2, axis=0).reshape(4 * LEAF, SUB)
    t3 = dot_blocks(g3, by_zy(ds))
    (t3_full,) = call(swap, [(4, LEAF, SUB)], sems(3) + [dma2], 3, t3)
    x3 = -dot_blocks(rows3, by_zy(t3_full.reshape(4 * LEAF, SUB)))

    (team_x,) = call(team_only, [(8, LEAF, SUB)], sems(9) + [dma2], 4, x3)
    d0 = team_d[0:2].reshape(4 * LEAF, SUB)
    d1 = team_d[2:4].reshape(4 * LEAF, SUB)
    x10s = jnp.concatenate([team_x[2], team_x[4], team_x[3], team_x[5]], axis=0)
    a_top = jnp.concatenate([d0, jnp.zeros_like(d0)], axis=1)
    a_bot = jnp.concatenate([x10s, d1], axis=1)
    a_mat = jnp.concatenate([a_top, a_bot], axis=0).reshape(2, RING, 2, 2 * SUB, 2 * SUB)
    a_blocks = jnp.stack([a_mat[0, :, 0], a_mat[1, :, 0], a_mat[1, :, 1], a_mat[0, :, 1]]).reshape(16, 2 * SUB, 2 * SUB)
    t4 = dot_blocks(g4, a_blocks)
    d2_rows = jnp.where(x == 2, lax.dynamic_index_in_dim(team_d, 4 + k, axis=0, keepdims=False)[:LEAF], hop)
    first_rows = jnp.where(inner, d2_rows, x3)
    team_t, rows4 = call(team_and_plane, [(8, LEAF, 2 * SUB), (RING, RING, LEAF, SUB)], sems(25) + [dma2], 5, t4, first_rows)
    rows4 = rows4.reshape(16, LEAF, SUB)
    t_first = jnp.concatenate([team_t[4], team_t[2], team_t[5], team_t[3]], axis=0)
    t_second = jnp.where(inner, 0.0, jnp.concatenate([team_t[6], team_t[0], team_t[7], team_t[1]], axis=0))
    x4 = -(dot_blocks(rows4, by_zy(t_first)) + dot_blocks(rows3, by_zy(t_second)))
    (out,) = call(place, [tile], [pltpu.SemaphoreType.DMA((3,)), pltpu.SemaphoreType.DMA((8,)), dma2], 6, dg, x3, x4)
    return out


def solution(mesh):
    grid = Mesh(mesh.devices.reshape(RING, RING, RING, 2), AXES)
    spec = P(("x", "core"), ("z", "y"))
    return jax.shard_map(invert, mesh=grid, in_specs=(spec,), out_specs=spec, check_vma=False)
```

time: 3280 us -> 375 us (0.11); the launches traced: 3240 us -> 368 us
  blocking collectives: 1080 us -> 0 us
  starting transfers between devices: 693 us -> 0.04 us
  other arithmetic: 666 us -> 6.78 us
  waiting for transfers between devices: 524 us -> 0.71 us
  Pallas kernels: 0 us -> 302 us
  local copies, waits for them, and re-layouts: 166 us -> 12.3 us
  matrix products: 90.4 us -> 31.8 us
    all_gather x64 -> x0, blocking collectives: 1080 us -> none  [the longest x24 545 us: summa_prod(): left_rows = lax.all_gather(left_tile, 'col', axis=1, tiled=True)]
    ppermute x300 -> x0, starting transfers between devices: 691 us -> none  [the longest x150 416 us: put_half(): slot_list.append(lax.ppermute(local_tile, axis_name, pair_list))]
    another operation x49 -> x1, other arithmetic: 655 us -> 2.36 us  [invert(): jnp.stack([a_mat[0, :, 0], a_mat[1, :, 0], a_mat[1, :, 1], a_mat[0, :, 1]])]
    ppermute x300 -> x0, waiting for transfers between devices: 365 us -> none  [the longest x150 296 us: take_half(): received.append(lax.ppermute(halves[half_idx], axis_name, pair_list))]
    pallas_call x0 -> x7, Pallas kernels: none -> 302 us  [call(): pl.pallas_call(kernel, out_shape=[jax.ShapeDtypeStruct(s, F32) for s in s...]
    all_gather x28 -> x2, waiting for transfers between devices: 159 us -> 0.01 us  [the longest x1 0.01 us: invert(): g3 = lax.all_gather(c3, ('z', 'y'), axis=0)]
    another operation x336 -> x1, local copies, waits for them, and re-layouts: 134 us -> 0.39 us  [invert(): jnp.stack([a_mat[0, :, 0], a_mat[1, :, 0], a_mat[1, :, 1], a_mat[0, :, 1]])]
  transfers between devices with their start and end apart: 328 -> 2, of which waited for: 87 -> 0; matrix products, arithmetic and copies ran while one was open for 28% -> 7% of each run, Pallas kernels for 0% -> 53%
where the time goes in v2:
time: 375 us; the launch traced here: 368 us
  Pallas kernels  302 us (81%)
  matrix products  31.8 us (8%)
  between operations  13.8 us (4%)
  local copies, waits for them, and re-layouts  12.3 us (3%)
  other arithmetic  6.78 us (2%)
    pallas_call x7, Pallas kernels, call(): pl.pallas_call(kernel, out_shape=[jax.ShapeDtypeStruct(s, F32) for s in s...  302 us
    dot_general x5, matrix products, dot_blocks(): lax.dot_general(left, right, (((0, 2), (0, 1)), ((), ())), precision=lax....  31.8 us
  transfers between devices with their start and end apart: 2, of which 0 were waited for; matrix products, arithmetic and copies ran while one was open for 7% of the time, Pallas kernels for 53%

profile of v2, /device:TPU:38, one launch (start us, length us, event | category | flops | bytes accessed | tf_op | source)
XLA Modules:
  0.0 367.6 jit_solution(17611908740468832223)
XLA Ops:
  6.5 0.0 all-gather.5.cloned.1.call-start
  6.5 30.6 %leaves.1 = (f32[512,512]{1,0:T(8,128)}, f32[512,512]{1,0:T(8,128)}, f32[512,512]{1,0:T(8,128)}, f32[512,512]{1,0:T(8,128)}, f32[1024,512]{1,0:T(8,128)}, /*index=5*/f32[512,128]{1,0:T(8,128)}, f32[512,256]{1,0:T(8,128)}) custom-call(f32[1024,512]{1,0:T(8,128)} %t_ref.3), custom_call_target="tpu_custom_call" | custom-call | tf_op jit(solution)/shard_map/leaves/pallas_call | solution.py:43
  37.1 0.0 all-gather.5.cloned.1.call-update
  37.1 0.0 all-gather.7.cloned.1.call-start
  37.2 0.7 all-gather.7.cloned.1.call-update
  37.9 12.0 %diagonal.1.dg = f32[1024,512]{1,0:T(8,128)} custom-call(f32[1024,512]{1,0:T(8,128)} %t_ref.3, f32[512,512]{1,0:T(8,128)} %get-tuple-element.17.inv, f32[512,512]{1,0:T(8,128)} %get-tuple-element.18.nb, f32[512,512]{1,0:T(8,128)} %get-tuple-element.19.near, f32[512,512]{1,0:T(8,128)} %get-tuple-element.20.l_next, f32[1024,512]{1,0:T(8,128)} %get-tuple-element.21.c_next), custom_call_target="tpu_custom_call" | custom-call | tf_op jit(solution)/shard_map/diagonal/pallas_call | solution.py:43
  49.9 154.3 %spread.1 = (f32[8,1024,128]{2,1,0:T(8,128)}, f32[512,128]{1,0:T(8,128)}, f32[4,4,512,128]{3,2,1,0:T(8,128)}) custom-call(f32[1024,512]{1,0:T(8,128)} %diagonal.1.dg), custom_call_target="tpu_custom_call" | custom-call | tf_op jit(solution)/shard_map/spread/pallas_call | solution.py:43
  204.2 2.1 fusion.23
  206.3 0.0 copy-start.2
  206.3 1.3 copy.11
  207.6 0.0 all-gather.5.cloned.1.call-done
  207.6 6.7 %convolution_bitcast_fusion.2.t_ref = f32[512,128]{1,0:T(8,128)} fusion(f32[16,128,128]{1,2,0:T(8,128)} %bitcast.120, f32[16,512,128]{2,1,0:T(8,128)} %bitcast.118), kind=kOutput, calls=%fused_computation.18 | convolution fusion | flops 1610612736 | bytes 5505024 | tf_op jit(solution)/shard_map/dot_general | solution.py:24
  214.2 10.8 %swap.1 = f32[4,512,128]{2,1,0:T(8,128)} custom-call(f32[512,128]{1,0:T(8,128)} %convolution_bitcast_fusion.2.t_ref), custom_call_target="tpu_custom_call" | custom-call | tf_op jit(solution)/shard_map/swap/pallas_call | solution.py:43
  225.1 0.0 copy-done.2
  225.1 6.7 %fusion.22 = (f32[512,128]{1,0:T(8,128)}, f32[512,128]{1,0:T(8,128)}) fusion(f32[512,128]{1,0:T(8,128)S(1)} %copy-done.2, f32[8,1024,128]{2,1,0:T(8,128)} %get-tuple-element.23, s32[]{:T(128)S(6)} %select_n.38, pred[]{:T(512)S(6)} %eq.8, pred[]{:T(512)S(6)} %or.3, f32[4,4,512,128]{3,2,1,0:T(8,128)} %get-tuple-element.22, f32[4,4,128,128]{3,2,1,0:T(8,128)} %bitcast.119), kind=kOutput, calls=%fused_computation.35 | convolution fusion | flops 1610809344 | bytes 6291462 | tf_op jit(solution)/shard_map/dot_general | solution.py:24
  231.8 19.3 %team_only.1 = f32[8,512,128]{2,1,0:T(8,128)} custom-call(f32[512,128]{1,0:T(8,128)} %get-tuple-element.49.tile.x3), custom_call_target="tpu_custom_call" | custom-call | tf_op jit(solution)/shard_map/team_only/pallas_call | solution.py:43
  251.1 1.3 slice_bitcast_fusion.15
  252.3 4.0 %select_maximum_fusion = f32[4096,256]{1,0:T(8,128)S(1)} fusion(f32[2048,128]{1,0:T(8,128)S(1)} %bitcast.116, f32[2048,128]{1,0:T(8,128)S(1)} %bitcast.115, f32[512,128]{1,0:T(8,128)S(1)} %get-tuple-element.45, f32[512,128]{1,0:T(8,128)S(1)} %get-tuple-element.46, f32[512,128]{1,0:T(8,128)S(1)} %get-tuple-element.47, f32[512,128]{1,0:T(8,128)S(1)} %get-tuple-element.44), kind=kLoop, calls=%fused_computation | loop fusion | flops 7340032 | bytes 7340032 | tf_op jit(solution)/shard_map/concatenate | solution.py:559
  256.4 0.4 slice_bitcast_fusion.3
  256.8 2.4 pad_maximum_fusion
  259.1 0.0 all-gather.7.cloned.1.call-done
  259.1 10.6 %convolution_bitcast_fusion.tile = f32[512,256]{1,0:T(8,128)} fusion(f32[16,256,256]{2,1,0:T(8,128)} %bitcast.110, f32[16,512,256]{2,1,0:T(8,128)} %bitcast.112), kind=kOutput, calls=%fused_computation.13 | convolution fusion | flops 6442450944 | bytes 13107200 | tf_op jit(solution)/shard_map/dot_general | solution.py:24
  269.8 41.0 %team_and_plane.1 = (f32[8,512,256]{2,1,0:T(8,128)}, f32[4,4,512,128]{3,2,1,0:T(8,128)}) custom-call(f32[512,256]{1,0:T(8,128)} %convolution_bitcast_fusion.tile, f32[512,128]{1,0:T(8,128)} %get-tuple-element.48.block), custom_call_target="tpu_custom_call" | custom-call | tf_op jit(solution)/shard_map/team_and_plane/pallas_call | solution.py:43
  310.8 2.4 slice_bitcast_fusion.7
  313.2 0.0 copy-start.1
  313.2 0.4 pad_maximum_fusion.1
  313.7 0.0 copy-start
  313.7 1.8 copy-done.1
  315.4 3.4 fusion.6
  318.9 0.0 copy-done
  318.9 4.3 %fusion.15.x4 = f32[512,256]{1,0:T(8,128)} fusion(f32[512,256]{1,0:T(8,128)S(1)} %fusion.6, f32[4,4,512,128]{3,2,1,0:T(8,128)S(1)} %copy-done, f32[4,4,128,256]{3,2,1,0:T(8,128)S(1)} %bitcast.113), kind=kOutput, calls=%fused_computation.15 | convolution fusion | flops 3221487616 | bytes 7340032 | tf_op jit(solution)/shard_map/dot_general | solution.py:24
  323.2 34.3 %place.1 = f32[1024,512]{1,0:T(8,128)} custom-call(f32[1024,512]{1,0:T(8,128)} %diagonal.1.dg, f32[512,128]{1,0:T(8,128)} %get-tuple-element.49.tile.x3, f32[512,256]{1,0:T(8,128)} %fusion.15.x4), custom_call_target="tpu_custom_call" | custom-call | tf_op jit(solution)/shard_map/place/pallas_call | solution.py:43
  357.5 3.1 copy.54
Async XLA Ops:
  6.5 201.0 %all-gather.5.cloned.1.call-start = ((), (), s32[]{:S(2)}) async-start(), calls=%async_computation | async-start | bytes 4456448 | tf_op jit(solution)/shard_map/all_gather | solution.py:541
  37.1 222.0 %all-gather.7.cloned.1.call-start = ((), (), s32[]{:S(2)}) async-start(), calls=%async_computation.1 | async-start | bytes 8912896 | tf_op jit(solution)/shard_map/all_gather | solution.py:542
  206.3 18.8 %copy-start.2 = (f32[512,128]{1,0:T(8,128)S(1)}, f32[512,128]{1,0:T(8,128)}, u32[]{:S(2)}) copy-start(f32[512,128]{1,0:T(8,128)} %get-tuple-element.26) | copy-start | bytes 786436
  313.2 2.2 copy-start.1
  313.7 5.2 %copy-start = (f32[4,4,512,128]{3,2,1,0:T(8,128)S(1)}, f32[4,4,512,128]{3,2,1,0:T(8,128)}, u32[]{:S(2)}) copy-start(f32[4,4,512,128]{3,2,1,0:T(8,128)} %get-tuple-element.22) | copy-start | bytes 12582916
Sparse Core Ops, SparseCore 0:
  37.2 62.7 all-gather.4
  102.2 98.4 all-gather.6
